TPU v7x, 8 devices: a whole 2x2x1 slice. The times are simulated.
8 devices in a mesh: rep: 1 (over z), dp: 8 (over x, y, core).
Axes of the slice: x: 2, y: 2, z: 1, core: 2. Of those that a mesh axis runs over, the one named last changes fastest.
Arguments:
- g_w_gate: bfloat16 [8, 2, 1280, 3584], P(('rep', 'dp'))
- g_w_up: bfloat16 [8, 2, 1280, 3584], P(('rep', 'dp'))
- g_w_down: bfloat16 [8, 2, 3584, 1280], P(('rep', 'dp'))
- w_gate: bfloat16 [2, 1280, 3584], replicated
- w_up: bfloat16 [2, 1280, 3584], replicated
- w_down: bfloat16 [2, 3584, 1280], replicated
- m_w_gate: float32 [2, 1280, 3584], P(None, 'dp')
- m_w_up: float32 [2, 1280, 3584], P(None, 'dp')
- m_w_down: float32 [2, 3584, 1280], P(None, 'dp')
- v_w_gate: float32 [2, 1280, 3584], P(None, 'dp')
- v_w_up: float32 [2, 1280, 3584], P(None, 'dp')
- v_w_down: float32 [2, 3584, 1280], P(None, 'dp')
Outputs:
- output 1: bfloat16 [2, 1280, 3584], P('rep')
- output 2: bfloat16 [2, 1280, 3584], P('rep')
- output 3: bfloat16 [2, 3584, 1280], P('rep')
- output 4: float32 [2, 1280, 3584], P('rep', 'dp')
- output 5: float32 [2, 1280, 3584], P('rep', 'dp')
- output 6: float32 [2, 3584, 1280], P('rep', 'dp')
- output 7: float32 [2, 1280, 3584], P('rep', 'dp')
- output 8: float32 [2, 1280, 3584], P('rep', 'dp')
- output 9: float32 [2, 3584, 1280], P('rep', 'dp')
All inputs are finite; a program needn't handle non-finite values.
Results may differ from a plain program's by a relative error of at most 0.022.
Values are sent between devices in bfloat16 or wider.
A program may use at most 2 GiB of HBM per device.

v0:
```python
import jax
import jax.numpy as jnp
from jax import lax
from jax.sharding import PartitionSpec as P


def adamw(w, m, v, g):
    m = 0.9 * m + 0.1 * g
    v = 0.95 * v + 0.05 * g * g
    step = m * lax.rsqrt(v + 1e-8) + 0.1 * w
    return (w - 0.02 * step).astype(jnp.bfloat16), m, v


def clipped(gradients, sum_of_squares, count):
    factor = jnp.minimum(1.0, 0.5 * lax.rsqrt(sum_of_squares / count + 1e-30))
    return [g * factor for g in gradients]


def solution(mesh):
    def step(*arrays):
        terms, weights, m, v = (arrays[i : i + 3] for i in (0, 3, 6, 9))
        gradients = [lax.psum_scatter(t[0], "dp", scatter_dimension=1, tiled=True).astype(jnp.float32) for t in terms]
        squares = lax.psum(sum(jnp.sum(g * g) for g in gradients), "dp")
        gradients = clipped(gradients, squares, lax.psum(1, "dp") * sum(g.size for g in gradients))
        me = lax.axis_index("dp")
        own = [lax.dynamic_slice_in_dim(w, me * one.shape[1], one.shape[1], 1).astype(jnp.float32) for w, one in zip(weights, m, strict=True)]
        new = [adamw(w, m, v, g) for w, m, v, g in zip(own, m, v, gradients, strict=True)]
        whole = [lax.all_gather(one[0], "dp", axis=1, tiled=True) for one in new]
        return (*whole, *(one[1] for one in new), *(one[2] for one in new))

    all_of, cut = P(None, None, None), P(None, "dp", None)
    return jax.shard_map(
        step,
        mesh=mesh,
        in_specs=(P(("rep", "dp"), None, None, None),) * 3 + (all_of,) * 3 + (cut,) * 6,
        out_specs=(P("rep", None, None),) * 3 + (P("rep", "dp", None),) * 6,
        check_vma=False,
    )
```

profile of v0, /device:TPU:0, one launch (start us, length us, event | category | flops | bytes accessed | tf_op | source)
XLA Modules:
  0.0 723.7 jit_solution(7203691224741042979)
XLA Ops:
  7.2 0.0 reduce-scatter.4.cloned.1.call-start
  7.2 0.7 reduce-scatter.4.cloned.1.call-update
  7.9 0.0 reduce-scatter.6.cloned.1.call-start
  8.0 0.7 reduce-scatter.6.cloned.1.call-update
  8.7 0.0 reduce-scatter.8.cloned.1.call-start
  8.7 0.7 reduce-scatter.8.cloned.1.call-update
  9.4 0.0 all-gather.8.cloned.1.call-start
  9.4 119.3 %reduce-scatter.4.cloned.1.call-done = bf16[2,160,3584]{2,1,0:T(8,128)(2,1)} async-done(((bf16[2,1280,3584]{2,1,0:T(8,128)(2,1)}), bf16[2,160,3584]{2,1,0:T(8,128)(2,1)}) %reduce-scatter.4.cloned.1.call-update) | async-done | bytes 2293776 | tf_op jit(solution)/shard_map/reduce_scatter | solution.py:22
  128.7 3.4 fusion.9
  132.2 114.5 %reduce-scatter.6.cloned.1.call-done = bf16[2,160,3584]{2,1,0:T(8,128)(2,1)} async-done(((bf16[2,1280,3584]{2,1,0:T(8,128)(2,1)}), bf16[2,160,3584]{2,1,0:T(8,128)(2,1)}) %reduce-scatter.6.cloned.1.call-update) | async-done | bytes 2293776 | tf_op jit(solution)/shard_map/reduce_scatter | solution.py:22
  246.6 3.4 fusion.10
  251.4 113.2 %reduce-scatter.8.cloned.1.call-done = bf16[2,448,1280]{2,1,0:T(8,128)(2,1)} async-done(((bf16[2,3584,1280]{2,1,0:T(8,128)(2,1)}), bf16[2,448,1280]{2,1,0:T(8,128)(2,1)}) %reduce-scatter.8.cloned.1.call-update) | async-done | bytes 2293776 | tf_op jit(solution)/shard_map/reduce_scatter | solution.py:22
  364.6 3.4 fusion.11
  368.7 22.2 %psum.7 = f32[]{:T(128)} all-reduce(f32[]{:T(128)S(6)} %add.65), channel_id=1, replica_groups=mesh['rep'=1,'dp'=8] {'dp'}, use_global_device_ids=true, to_apply=%region_6.0 | all-reduce | flops 1 | bytes 8 | tf_op jit(solution)/shard_map/psum | solution.py:23
  391.6 9.2 %fusion.17 = (bf16[2,448,1280]{2,1,0:T(8,128)(2,1)}, f32[2,448,1280]{2,1,0:T(8,128)}, f32[2,448,1280]{2,1,0:T(8,128)}) fusion(bf16[2,3584,1280]{2,1,0:T(8,128)(2,1)} %param.17, s32[]{:T(128)S(6)} %select_n.8, f32[]{:T(128)S(6)} %min_shard_map.3, bf16[2,448,1280]{2,1,0:T(8,128)(2,1)} %reduce-scatter.8.cloned.1.call-done, f32[2,448,1280]{2,1,0:T(8,128)} %param.23, ...), kind=kLoop, calls=%fused_computation.32 | loop fusion | flops 19496960 | bytes 25231368 | tf_op jit(solution)/shard_map/convert_element_type | solution.py:11
  400.8 0.0 all-gather.8.cloned.1.call-update
  400.9 0.0 all-gather.4.cloned.1.call-start
  400.9 0.0 copy-start.1
  400.9 9.4 %fusion.8 = (bf16[2,160,3584]{2,1,0:T(8,128)(2,1)}, f32[2,160,3584]{2,1,0:T(8,128)}, f32[2,160,3584]{2,1,0:T(8,128)}) fusion(bf16[2,1280,3584]{2,1,0:T(8,128)(2,1)} %param.15, s32[]{:T(128)S(6)} %select_n.7, f32[]{:T(128)S(6)} %min_shard_map.3, bf16[2,160,3584]{2,1,0:T(8,128)(2,1)} %reduce-scatter.4.cloned.1.call-done, f32[2,160,3584]{2,1,0:T(8,128)} %param.21, ...), kind=kLoop, calls=%fused_computation.23 | loop fusion | flops 19496960 | bytes 25231368 | tf_op jit(solution)/shard_map/convert_element_type | solution.py:11
  410.3 0.0 all-gather.4.cloned.1.call-update
  410.3 0.0 all-gather.6.cloned.1.call-start
  410.4 0.0 copy-done.1
  410.4 7.8 %fusion.14 = (bf16[2,160,3584]{2,1,0:T(8,128)(2,1)}, f32[2,160,3584]{2,1,0:T(8,128)}, f32[2,160,3584]{2,1,0:T(8,128)}) fusion(bf16[2,1280,3584]{2,1,0:T(8,128)(2,1)} %param.16, s32[]{:T(128)S(6)} %select_n.7, f32[]{:T(128)S(6)} %min_shard_map.3, bf16[2,160,3584]{2,1,0:T(8,128)(2,1)S(1)} %copy-done.1, f32[2,160,3584]{2,1,0:T(8,128)} %param.22, ...), kind=kLoop, calls=%fused_computation.29 | loop fusion | flops 19496960 | bytes 25231368 | tf_op jit(solution)/shard_map/convert_element_type | solution.py:11
  418.1 0.0 all-gather.6.cloned.1.call-update
  418.2 75.5 %all-gather.8.cloned.1.call-done = bf16[2,3584,1280]{2,1,0:T(8,128)(2,1)} async-done(((bf16[2,448,1280]{2,1,0:T(8,128)(2,1)}), bf16[2,3584,1280]{2,1,0:T(8,128)(2,1)}) %all-gather.8.cloned.1.call-update) | async-done | bytes 18350096 | tf_op jit(solution)/shard_map/all_gather | solution.py:28
  493.7 93.0 %all-gather.4.cloned.1.call-done = bf16[2,1280,3584]{2,1,0:T(8,128)(2,1)} async-done(((bf16[2,160,3584]{2,1,0:T(8,128)(2,1)}), bf16[2,1280,3584]{2,1,0:T(8,128)(2,1)}) %all-gather.4.cloned.1.call-update) | async-done | bytes 18350096 | tf_op jit(solution)/shard_map/all_gather | solution.py:28
  586.7 93.0 %all-gather.6.cloned.1.call-done = bf16[2,1280,3584]{2,1,0:T(8,128)(2,1)} async-done(((bf16[2,160,3584]{2,1,0:T(8,128)(2,1)}), bf16[2,1280,3584]{2,1,0:T(8,128)(2,1)}) %all-gather.6.cloned.1.call-update) | async-done | bytes 18350096 | tf_op jit(solution)/shard_map/all_gather | solution.py:28
  679.7 0.0 copy-start
  679.7 0.0 slice-start
  679.7 0.0 slice-start.1
  679.7 0.0 slice-start.2
  679.8 19.7 %copy.24 = bf16[2,1280,3584]{2,1,0:T(8,128)(2,1)} copy(bf16[2,1280,3584]{2,1,0:T(8,128)(2,1)} %all-gather.4.cloned.1.call-done) | data formatting | bytes 36700160
  699.4 0.0 copy-done
  699.4 0.0 slice-start.3
  699.4 0.0 slice-start.4
  699.4 9.3 %copy.25 = bf16[2,1280,3584]{2,1,0:T(8,128)(2,1)} copy(bf16[2,1280,3584]{2,1,0:T(8,128)(2,1)S(1)} %copy-done) | data formatting | bytes 36700160
  708.7 0.0 slice-done
  708.7 0.0 slice-done.1
  708.7 0.0 slice-done.2
  708.7 0.5 slice-done.3
  709.2 0.9 slice-done.4
  710.2 6.7 copy.26
  (1 shorter events, 0.0 us)
Async XLA Ops:
  7.2 121.6 %reduce-scatter.4.cloned.1.call-start = ((), (), s32[]{:S(2)}) async-start(), calls=%async_computation.3 | async-start | bytes 20643840 | tf_op jit(solution)/shard_map/reduce_scatter | solution.py:22
  7.9 238.7 %reduce-scatter.6.cloned.1.call-start = ((), (), s32[]{:S(2)}) async-start(), calls=%async_computation.4 | async-start | bytes 20643840 | tf_op jit(solution)/shard_map/reduce_scatter | solution.py:22
  8.7 355.9 %reduce-scatter.8.cloned.1.call-start = ((), (), s32[]{:S(2)}) async-start(), calls=%async_computation.5 | async-start | bytes 20643840 | tf_op jit(solution)/shard_map/reduce_scatter | solution.py:22
  9.4 484.3 %all-gather.8.cloned.1.call-start = ((), (), s32[]{:S(2)}) async-start(), calls=%async_computation.8 | async-start | bytes 20643840 | tf_op jit(solution)/shard_map/all_gather | solution.py:28
  400.9 185.8 %all-gather.4.cloned.1.call-start = ((), (), s32[]{:S(2)}) async-start(), calls=%async_computation.6 | async-start | bytes 20643840 | tf_op jit(solution)/shard_map/all_gather | solution.py:28
  400.9 9.5 %copy-start.1 = (bf16[2,160,3584]{2,1,0:T(8,128)(2,1)S(1)}, bf16[2,160,3584]{2,1,0:T(8,128)(2,1)}, u32[]{:S(2)}) copy-start(bf16[2,160,3584]{2,1,0:T(8,128)(2,1)} %reduce-scatter.6.cloned.1.call-done) | copy-start | bytes 6881284
  410.3 269.4 %all-gather.6.cloned.1.call-start = ((), (), s32[]{:S(2)}) async-start(), calls=%async_computation.7 | async-start | bytes 20643840 | tf_op jit(solution)/shard_map/all_gather | solution.py:28
  679.7 19.7 %copy-start = (bf16[2,1280,3584]{2,1,0:T(8,128)(2,1)S(1)}, bf16[2,1280,3584]{2,1,0:T(8,128)(2,1)}, u32[]{:S(2)}) copy-start(bf16[2,1280,3584]{2,1,0:T(8,128)(2,1)} %all-gather.6.cloned.1.call-done) | copy-start | bytes 55050244
  679.7 29.0 %slice-start = ((s8[18350080]{0:T(1024)(128)(4,1)}), s8[4194304]{0:T(1024)(128)(4,1)S(1)}, s32[]{:S(2)}) async-start(s8[18350080]{0:T(1024)(128)(4,1)} %bitcast.6), calls=%async_computation.9 | async-start | bytes 8388608
  679.7 29.0 %slice-start.1 = ((s8[18350080]{0:T(1024)(128)(4,1)}), s8[4194304]{0:T(1024)(128)(4,1)S(1)}, s32[]{:S(2)}) async-start(s8[18350080]{0:T(1024)(128)(4,1)} %bitcast.6), calls=%async_computation.10 | async-start | bytes 8388608
  679.7 29.0 %slice-start.2 = ((s8[18350080]{0:T(1024)(128)(4,1)}), s8[4194304]{0:T(1024)(128)(4,1)S(1)}, s32[]{:S(2)}) async-start(s8[18350080]{0:T(1024)(128)(4,1)} %bitcast.6), calls=%async_computation.11 | async-start | bytes 8388608
  699.4 9.8 %slice-start.3 = ((s8[18350080]{0:T(1024)(128)(4,1)}), s8[4194304]{0:T(1024)(128)(4,1)S(1)}, s32[]{:S(2)}) async-start(s8[18350080]{0:T(1024)(128)(4,1)} %bitcast.6), calls=%async_computation.12 | async-start | bytes 8388608
  699.4 10.7 %slice-start.4 = ((s8[18350080]{0:T(1024)(128)(4,1)}), s8[1572864]{0:T(1024)(128)(4,1)S(1)}, s32[]{:S(2)}) async-start(s8[18350080]{0:T(1024)(128)(4,1)} %bitcast.6), calls=%async_computation.13 | async-start | bytes 3145728
Sparse Core Ops, SparseCore 0:
  11.6 117.0 reduce-scatter.3
  132.4 114.2 reduce-scatter.5
  250.3 114.2 reduce-scatter.7
  401.0 92.6 all-gather.7
  495.9 90.7 all-gather.3
  589.0 90.7 all-gather.5
where the time goes:
time: 724 us
  waiting for transfers between devices  611 us (84%)
  local copies, waits for them, and re-layouts  37.1 us (5%)
  other arithmetic  36.7 us (5%)
  blocking collectives  22.2 us (3%)
  between operations  16.8 us (2%)
    reduce_scatter x3, waiting for transfers between devices, step(): lax.psum_scatter(t[0], 'dp', scatter_dimension=1, tiled=True)  347 us
    all_gather x3, waiting for transfers between devices, step(): whole = [lax.all_gather(one[0], 'dp', axis=1, tiled=True) for one in new]  262 us
    unnamed x17, local copies, waits for them, and re-layouts  37.1 us
    convert_element_type x3, other arithmetic, adamw(): return ((w - 0.02 * step).astype(jnp.bfloat16), m, v)  26.4 us
    psum x1, blocking collectives, step(): squares = lax.psum(sum((jnp.sum(g * g) for g in gradients)), 'dp')  22.2 us
  transfers between devices with their start and end apart: 6, of which 6 were waited for; matrix products, arithmetic and copies ran while one was open for 3% of the time, Pallas kernels for 0%

commit v1 on v0

v1 whole, which is shorter than its diff:
```python
import functools

import jax
import jax.numpy as jnp
from jax import lax
from jax.experimental import pallas as pl
from jax.experimental.pallas import tpu as pltpu
from jax.sharding import PartitionSpec as P

MESH = pl.DeviceIdType.MESH
DEVICES = 8
CHIPS = 4
SPLIT = 4
SLOTS = 5
LANES = 128


def adamw(w, m, v, g):
    m = 0.9 * m + 0.1 * g
    v = 0.95 * v + 0.05 * g * g
    step = m * lax.rsqrt(v + 1e-8) + 0.1 * w
    return (w - 0.02 * step).astype(jnp.bfloat16), m, v


def tiled(a):
    *lead, rows, columns = a.shape
    a = a.reshape(*lead, rows // 8, 8, columns // LANES, LANES)
    return jnp.swapaxes(a, -3, -2).reshape(*lead, rows * columns // LANES, LANES)


def untiled(a, rows, columns):
    lead = a.shape[:-2]
    a = a.reshape(*lead, rows // 8, columns // LANES, 8, LANES)
    return jnp.swapaxes(a, -3, -2).reshape(*lead, rows, columns)


def place():
    me = lax.axis_index("dp")
    core = lax.rem(me, 2)
    x, y = me // 4, lax.rem(me // 2, 2)
    return me, core, x, y


def scatter_kernel(units, half, chunk, layers, *refs):
    terms, (grads, total_ref), scratch = refs[:3], (refs[3:6], refs[6]), refs[7:]
    own, part, sx, sy, sx2, sy2, rx, ry, rx2, ry2, done, acc, sums = scratch[:13]
    own_sem, part_send, part_recv, credit, sx_sem, sy_sem, sx2_sem, sy2_sem = scratch[13:21]
    rx_sem, ry_sem, rx2_sem, ry2_sem, out_sem, sum_send, sum_recv = scratch[21:]
    me, core, x, y = place()
    px, py, pc = me + 4 - 8 * x, me + 2 - 4 * y, me + 1 - 2 * core
    here, beside_y, beside_x, across = 2 * x + y, 2 * x + 1 - y, 2 - 2 * x + y, 3 - 2 * x - y
    a_rows, b_rows = pl.ds(0, half), pl.ds(half, half)
    steps = half // chunk

    barrier = pltpu.get_barrier_semaphore()
    for k in range(1, DEVICES):
        pl.semaphore_signal(barrier, inc=1, device_id={"dp": lax.rem(me + k, DEVICES)}, device_id_type=MESH)
    pl.semaphore_wait(barrier, DEVICES - 1)

    def remote(src, dst, send, recv, to):
        return pltpu.make_async_remote_copy(src_ref=src, dst_ref=dst, send_sem=send, recv_sem=recv, device_id={"dp": to}, device_id_type=MESH)

    def where(u):
        t = u // 3
        return t // SPLIT, pl.ds(pl.multiple_of(lax.rem(t, SPLIT) * 2 * half, 16), 2 * half)

    def loads(u, term):
        layer, rows = where(u)
        slot = lax.rem(u, SLOTS)
        mine = pltpu.make_async_copy(term.at[layer, :, core, rows], own.at[slot], own_sem.at[slot])
        other = remote(term.at[layer, :, 1 - core, rows], part.at[slot], part_send.at[slot], part_recv.at[slot], pc)
        return mine, other

    def prefetch(u):
        @pl.when(u >= SLOTS)
        def _():
            pl.semaphore_wait(credit, 1)

        for k in range(3):

            @pl.when(lax.rem(u, 3) == k)
            def _():
                for copy in loads(u, terms[k]):
                    copy.start()

    def first_x(u):
        return remote(sx.at[lax.rem(u, 2)], rx.at[u], sx_sem.at[lax.rem(u, 2)], rx_sem.at[u], px)

    def first_y(u):
        return remote(sy.at[lax.rem(u, 2)], ry.at[u], sy_sem.at[lax.rem(u, 2)], ry_sem.at[u], py)

    def second_x(u):
        return remote(sx2.at[lax.rem(u, 2)], rx2.at[u], sx2_sem.at[lax.rem(u, 2)], rx2_sem.at[u], px)

    def second_y(u):
        return remote(sy2.at[lax.rem(u, 2)], ry2.at[u], sy2_sem.at[lax.rem(u, 2)], ry2_sem.at[u], py)

    def store(u, grad):
        layer, rows = where(u)
        return pltpu.make_async_copy(done.at[lax.rem(u, 2)], grad.at[layer, rows], out_sem.at[lax.rem(u, 2)])

    def pair(slot, chip, rows):
        return own[slot, chip, rows].astype(jnp.float32) + part[slot, chip, rows].astype(jnp.float32)

    def at(base, s):
        return pl.ds(pl.multiple_of(base + s * chunk, 16), chunk)

    def stage1(u):
        slot, two = lax.rem(u, SLOTS), lax.rem(u, 2)
        mine, other = loads(u, terms[0])
        mine.wait()
        other.wait()

        @pl.when(u >= 2)
        def _():
            first_x(u - 2).wait_send()
            first_y(u - 2).wait_send()

        def go(s, _):
            for n, chip in enumerate((beside_x, across)):
                sx[two, n, at(0, s)] = pair(slot, chip, at(0, s)).astype(jnp.bfloat16)
            for n, chip in enumerate((beside_y, across)):
                sy[two, n, at(0, s)] = pair(slot, chip, at(half, s)).astype(jnp.bfloat16)
            return 0

        lax.fori_loop(0, steps, go, 0)
        first_x(u).start()
        first_y(u).start()

    def stage2(u):
        slot, two = lax.rem(u, SLOTS), lax.rem(u, 2)
        first_x(u).wait_recv()
        first_y(u).wait_recv()

        @pl.when(u >= 2)
        def _():
            second_x(u - 2).wait_send()
            second_y(u - 2).wait_send()

        def go(s, _):
            r = at(0, s)
            sy2[two, r] = (pair(slot, beside_y, r) + rx[u, 1, r].astype(jnp.float32)).astype(jnp.bfloat16)
            sx2[two, r] = (pair(slot, beside_x, at(half, s)) + ry[u, 1, r].astype(jnp.float32)).astype(jnp.bfloat16)
            return 0

        lax.fori_loop(0, steps, go, 0)
        second_x(u).start()
        second_y(u).start()

    def stage3(u):
        slot, two = lax.rem(u, SLOTS), lax.rem(u, 2)
        second_x(u).wait_recv()
        second_y(u).wait_recv()

        @pl.when(u >= 2)
        def _():
            store(u - 2, grads[0]).wait()

        def go(s, sums):
            r = at(0, s)
            for base, near, far in ((0, rx, ry2), (half, ry, rx2)):
                g = pair(slot, here, at(base, s)) + near[u, 0, r].astype(jnp.float32) + far[u, r].astype(jnp.float32)
                g = g.astype(jnp.bfloat16)
                done[two, at(base, s)] = g
                g = g.astype(jnp.float32)
                sums = sums + jnp.sum((g * g).reshape(chunk // 8, 8, LANES), axis=0)
            return sums

        acc[...] += lax.fori_loop(0, steps, go, jnp.zeros((8, LANES), jnp.float32))
        for k in range(3):

            @pl.when(lax.rem(u, 3) == k)
            def _():
                store(u, grads[k]).start()

        @pl.when(u + SLOTS < units)
        def _():
            pl.semaphore_signal(credit, inc=1, device_id={"dp": pc}, device_id_type=MESH)

    acc[...] = jnp.zeros_like(acc)
    prefetch(0)
    prefetch(1)

    def body(i, _):
        @pl.when(i < units)
        def _():
            stage1(i)

        @pl.when(i + 2 < units)
        def _():
            prefetch(i + 2)

        @pl.when(jnp.logical_and(i >= 1, i <= units))
        def _():
            stage2(i - 1)

        @pl.when(i >= 2)
        def _():
            stage3(i - 2)

        return 0

    lax.fori_loop(0, units + 2, body, 0)

    def share(k):
        to = lax.rem(me + k, DEVICES)
        return remote(acc, sums.at[me], sum_send.at[k], sum_recv.at[me], to)

    for k in range(1, DEVICES):
        share(k).start()
    sums[me] = acc[...]
    for u in (units - 2, units - 1):
        first_x(u).wait_send()
        first_y(u).wait_send()
        second_x(u).wait_send()
        second_y(u).wait_send()
        store(u, grads[0]).wait()
    for k in range(1, DEVICES):
        source = lax.rem(me + k, DEVICES)
        remote(acc, sums.at[source], sum_send.at[k], sum_recv.at[source], source).wait()
    total = sums[0]
    for d in range(1, DEVICES):
        total = total + sums[d]
    total_ref[...] = total


def scatter(terms):
    layers, rows, _ = terms[0].shape
    block = rows // DEVICES
    half = block // (2 * SPLIT)
    units = 3 * layers * SPLIT
    terms = [t.reshape(layers, CHIPS, 2, block, LANES) for t in terms]
    bf = functools.partial(pltpu.VMEM, dtype=jnp.bfloat16)
    dma = pltpu.SemaphoreType.DMA
    hbm = pl.BlockSpec(memory_space=pl.ANY)
    *grads, total = pl.pallas_call(
        functools.partial(scatter_kernel, units, half, 112, layers),
        out_shape=[jax.ShapeDtypeStruct((layers, block, LANES), jnp.bfloat16)] * 3 + [jax.ShapeDtypeStruct((8, LANES), jnp.float32)],
        in_specs=[hbm] * 3,
        out_specs=[hbm] * 3 + [pl.BlockSpec(memory_space=pltpu.VMEM)],
        scratch_shapes=[
            bf((SLOTS, CHIPS, 2 * half, LANES)),
            bf((SLOTS, CHIPS, 2 * half, LANES)),
            bf((2, 2, half, LANES)),
            bf((2, 2, half, LANES)),
            bf((2, half, LANES)),
            bf((2, half, LANES)),
            bf((units, 2, half, LANES)),
            bf((units, 2, half, LANES)),
            bf((units, half, LANES)),
            bf((units, half, LANES)),
            bf((2, 2 * half, LANES)),
            pltpu.VMEM((8, LANES), jnp.float32),
            pltpu.VMEM((DEVICES, 8, LANES), jnp.float32),
            dma((SLOTS,)),
            dma((SLOTS,)),
            dma((SLOTS,)),
            pltpu.SemaphoreType.REGULAR,
            dma((2,)),
            dma((2,)),
            dma((2,)),
            dma((2,)),
            dma((units,)),
            dma((units,)),
            dma((units,)),
            dma((units,)),
            dma((2,)),
            dma((DEVICES,)),
            dma((DEVICES,)),
        ],
        compiler_params=pltpu.CompilerParams(collective_id=0, has_side_effects=True, vmem_limit_bytes=56 << 20),
        name="scatter",
    )(*terms)
    return grads, total


def solution(mesh):
    def step(*arrays):
        terms, weights, m, v = (arrays[i : i + 3] for i in (0, 3, 6, 9))
        shapes = [one.shape[1:] for one in weights]
        terms, weights, m, v = ([tiled(a) for a in arrays] for arrays in ([t[0] for t in terms], weights, m, v))
        grads, total = scatter(terms)
        count = DEVICES * sum(g.size for g in grads)
        factor = jnp.minimum(1.0, 0.5 * lax.rsqrt(jnp.sum(total) / count + 1e-30))
        me = lax.axis_index("dp")
        own = [lax.dynamic_slice_in_dim(w, me * one.shape[1], one.shape[1], 1).astype(jnp.float32) for w, one in zip(weights, m, strict=True)]
        new = [adamw(w, m, v, g.astype(jnp.float32) * factor) for w, m, v, g in zip(own, m, v, grads, strict=True)]
        whole = [lax.all_gather(one[0], "dp", axis=1, tiled=True) for one in new]
        whole = [untiled(w, *shape) for w, shape in zip(whole, shapes, strict=True)]
        moments = [untiled(one[k], shape[0] // DEVICES, shape[1]) for k in (1, 2) for one, shape in zip(new, shapes, strict=True)]
        return (*whole, *moments)

    all_of, cut = P(None, None, None), P(None, "dp", None)
    return jax.shard_map(
        step,
        mesh=mesh,
        in_specs=(P(("rep", "dp"), None, None, None),) * 3 + (all_of,) * 3 + (cut,) * 6,
        out_specs=(P("rep", None, None),) * 3 + (P("rep", "dp", None),) * 6,
        check_vma=False,
    )
```

time: 724 us -> 582 us (0.80)
  waiting for transfers between devices: 611 us -> 254 us
  Pallas kernels: 0 us -> 235 us
  blocking collectives: 22.2 us -> 0 us
    reduce_scatter x3 -> x0, waiting for transfers between devices: 347 us -> none  [step(): lax.psum_scatter(t[0], 'dp', scatter_dimension=1, tiled=True)]
    pallas_call x0 -> x1, Pallas kernels: none -> 235 us  [scatter(): pl.pallas_call(functools.partial(scatter_kernel, units, half, 112, layers...]
    psum x1 -> x0, blocking collectives: 22.2 us -> none  [step(): squares = lax.psum(sum((jnp.sum(g * g) for g in gradients)), 'dp')]
    mul x0 -> x6, other arithmetic: none -> 18.7 us  [the longest x3 10.4 us: adamw(): m = 0.9 * m + 0.1 * g]
    reduce_sum x3 -> x1, other arithmetic: 10.3 us -> 1.29 us  [step(): factor = jnp.minimum(1.0, 0.5 * lax.rsqrt(jnp.sum(total) / count + 1e-30))]
    all_gather x3, waiting for transfers between devices: 262 us -> 254 us  [step(): whole = [lax.all_gather(one[0], 'dp', axis=1, tiled=True) for one in new]]
    unnamed x17 -> x21, local copies, waits for them, and re-layouts: 37.1 us -> 37.4 us
  transfers between devices with their start and end apart: 6 -> 3, of which waited for: 6 -> 3; matrix products, arithmetic and copies ran while one was open for 3% -> 4% of each run, Pallas kernels for 0% -> 0%
where the time goes in v1:
time: 582 us
  waiting for transfers between devices  254 us (44%)
  Pallas kernels  235 us (40%)
  other arithmetic  41.3 us (7%)
  local copies, waits for them, and re-layouts  37.4 us (6%)
  between operations  14.5 us (2%)
    all_gather x3, waiting for transfers between devices, step(): whole = [lax.all_gather(one[0], 'dp', axis=1, tiled=True) for one in new]  254 us
    pallas_call x1, Pallas kernels, scatter(): pl.pallas_call(functools.partial(scatter_kernel, units, half, 112, layers...  235 us
    unnamed x21, local copies, waits for them, and re-layouts  37.4 us
    convert_element_type x3, other arithmetic, adamw(): return ((w - 0.02 * step).astype(jnp.bfloat16), m, v)  21.3 us
  transfers between devices with their start and end apart: 3, of which 3 were waited for; matrix products, arithmetic and copies ran while one was open for 4% of the time, Pallas kernels for 0%

profile of v1, /device:TPU:0, one launch (start us, length us, event | category | flops | bytes accessed | tf_op | source)
XLA Modules:
  0.0 582.1 jit_solution(3120366885680316034)
XLA Ops:
  7.2 0.0 all-gather.4.cloned.1.call-start
  7.2 0.0 copy-start.1
  7.2 5.0 broadcast_multiply_fusion.5
  12.2 0.0 copy-done.1
  12.2 2.5 broadcast_multiply_fusion.3
  14.8 235.1 %scatter.1 = (bf16[2,4480,128]{2,1,0:T(8,128)(2,1)}, bf16[2,4480,128]{2,1,0:T(8,128)(2,1)}, bf16[2,4480,128]{2,1,0:T(8,128)(2,1)}, f32[8,128]{1,0:T(8,128)}) custom-call(bf16[2,4,2,4480,128]{4,3,2,1,0:T(8,128)(2,1)} %bitcast.116, bf16[2,4,2,4480,128]{4,3,2,1,0:T(8,128)(2,1)} %bitcast.117, bf16[2,4,2,4480,128]{4,3,2,1,0:T(8,128)(2,1)} %bitcast.118), custom_call_target="tpu_custom_call" | custom-call | tf_op jit(solution)/shard_map/scatter/pallas_call | solution.py:236
  249.9 1.3 reduce_sum.9
  251.9 9.2 %fusion.2 = (bf16[2,4480,128]{2,1,0:T(8,128)(2,1)}, f32[2,4480,128]{2,1,0:T(8,128)}, f32[2,4480,128]{2,1,0:T(8,128)}) fusion(bf16[2,35840,128]{2,1,0:T(8,128)(2,1)} %bitcast.125, s32[]{:T(128)S(6)} %select_n.2, f32[2,4480,128]{2,1,0:T(8,128)} %bitcast.106, f32[]{:T(128)S(6)} %min_shard_map.3, bf16[2,4480,128]{2,1,0:T(8,128)(2,1)} %get-tuple-element.13, ...), kind=kLoop, calls=%fused_computation.11 | loop fusion | flops 17203200 | bytes 25231368 | tf_op jit(solution)/shard_map/convert_element_type | solution.py:22
  261.2 0.0 all-gather.4.cloned.1.call-update
  261.2 0.0 all-gather.6.cloned.1.call-start
  261.2 2.7 broadcast_multiply_fusion.4
  264.0 0.0 copy-start.3
  264.0 2.9 broadcast_multiply_fusion.2
  266.8 0.2 copy-done.3
  267.0 6.0 %fusion.5 = (bf16[2,4480,128]{2,1,0:T(8,128)(2,1)}, f32[2,4480,128]{2,1,0:T(8,128)}, f32[2,4480,128]{2,1,0:T(8,128)}) fusion(bf16[2,35840,128]{2,1,0:T(8,128)(2,1)} %bitcast.126, s32[]{:T(128)S(6)} %select_n.2, f32[2,4480,128]{2,1,0:T(8,128)S(1)} %bitcast.110, f32[]{:T(128)S(6)} %min_shard_map.3, bf16[2,4480,128]{2,1,0:T(8,128)(2,1)S(1)} %copy-done.3, ...), kind=kLoop, calls=%fused_computation.14 | loop fusion | flops 17203200 | bytes 25231368 | tf_op jit(solution)/shard_map/convert_element_type | solution.py:22
  273.0 0.0 all-gather.6.cloned.1.call-update
  273.0 0.0 all-gather.8.cloned.1.call-start
  273.1 2.7 broadcast_multiply_fusion.1
  275.8 0.0 copy-start.2
  275.8 2.8 broadcast_multiply_fusion
  278.7 0.2 copy-done.2
  278.8 6.0 %fusion.8 = (bf16[2,4480,128]{2,1,0:T(8,128)(2,1)}, f32[2,4480,128]{2,1,0:T(8,128)}, f32[2,4480,128]{2,1,0:T(8,128)}) fusion(bf16[2,35840,128]{2,1,0:T(8,128)(2,1)} %bitcast.127, s32[]{:T(128)S(6)} %select_n.2, f32[2,4480,128]{2,1,0:T(8,128)S(1)} %bitcast.108, f32[]{:T(128)S(6)} %min_shard_map.3, bf16[2,4480,128]{2,1,0:T(8,128)(2,1)S(1)} %copy-done.2, ...), kind=kLoop, calls=%fused_computation.17 | loop fusion | flops 17203200 | bytes 25231368 | tf_op jit(solution)/shard_map/convert_element_type | solution.py:22
  284.9 0.0 all-gather.8.cloned.1.call-update
  284.9 67.2 %all-gather.4.cloned.1.call-done = bf16[2,35840,128]{2,1,0:T(8,128)(2,1)} async-done(((bf16[2,4480,128]{2,1,0:T(8,128)(2,1)}), bf16[2,35840,128]{2,1,0:T(8,128)(2,1)}) %all-gather.4.cloned.1.call-update) | async-done | bytes 18350096 | tf_op jit(solution)/shard_map/all_gather | solution.py:288
  352.1 93.2 %all-gather.6.cloned.1.call-done = bf16[2,35840,128]{2,1,0:T(8,128)(2,1)} async-done(((bf16[2,4480,128]{2,1,0:T(8,128)(2,1)}), bf16[2,35840,128]{2,1,0:T(8,128)(2,1)}) %all-gather.6.cloned.1.call-update) | async-done | bytes 18350096 | tf_op jit(solution)/shard_map/all_gather | solution.py:288
  445.3 93.2 %all-gather.8.cloned.1.call-done = bf16[2,35840,128]{2,1,0:T(8,128)(2,1)} async-done(((bf16[2,4480,128]{2,1,0:T(8,128)(2,1)}), bf16[2,35840,128]{2,1,0:T(8,128)(2,1)}) %all-gather.8.cloned.1.call-update) | async-done | bytes 18350096 | tf_op jit(solution)/shard_map/all_gather | solution.py:288
  538.5 0.0 copy-start
  538.5 0.0 slice-start
  538.5 0.0 slice-start.1
  538.5 0.0 slice-start.2
  538.5 19.7 %copy.24 = bf16[2,1280,3584]{2,1,0:T(8,128)(2,1)} copy(bf16[2,1280,3584]{2,1,0:T(8,128)(2,1)} %bitcast.111) | data formatting | bytes 36700160
  558.2 0.0 copy-done
  558.2 0.0 slice-start.3
  558.2 0.0 slice-start.4
  558.2 9.3 %copy.25 = bf16[2,1280,3584]{2,1,0:T(8,128)(2,1)} copy(bf16[2,1280,3584]{2,1,0:T(8,128)(2,1)S(1)} %bitcast.112) | data formatting | bytes 36700160
  567.5 0.0 slice-done
  567.5 0.0 slice-done.1
  567.5 0.0 slice-done.2
  567.5 0.5 slice-done.3
  567.9 0.9 slice-done.4
  568.9 6.7 %copy.26 = bf16[2,3584,1280]{2,1,0:T(8,128)(2,1)} copy(bf16[2,3584,1280]{2,1,0:T(8,128)(2,1)S(1)} %bitcast.115) | data formatting | bytes 36700160
  (1 shorter events, 0.0 us)
Async XLA Ops:
  7.2 344.9 %all-gather.4.cloned.1.call-start = ((), (), s32[]{:S(2)}) async-start(), calls=%async_computation | async-start | bytes 20643840 | tf_op jit(solution)/shard_map/all_gather | solution.py:288
  7.2 5.0 copy-start.1
  261.2 184.1 %all-gather.6.cloned.1.call-start = ((), (), s32[]{:S(2)}) async-start(), calls=%async_computation.1 | async-start | bytes 20643840 | tf_op jit(solution)/shard_map/all_gather | solution.py:288
  264.0 3.0 copy-start.3
  273.0 265.4 %all-gather.8.cloned.1.call-start = ((), (), s32[]{:S(2)}) async-start(), calls=%async_computation.2 | async-start | bytes 20643840 | tf_op jit(solution)/shard_map/all_gather | solution.py:288
  275.8 3.0 copy-start.2
  538.5 19.7 %copy-start = (bf16[2,35840,128]{2,1,0:T(8,128)(2,1)S(1)}, bf16[2,35840,128]{2,1,0:T(8,128)(2,1)}, u32[]{:S(2)}) copy-start(bf16[2,35840,128]{2,1,0:T(8,128)(2,1)} %all-gather.6.cloned.1.call-done) | copy-start | bytes 55050244
  538.5 29.0 %slice-start = ((s8[18350080]{0:T(1024)(128)(4,1)}), s8[4194304]{0:T(1024)(128)(4,1)S(1)}, s32[]{:S(2)}) async-start(s8[18350080]{0:T(1024)(128)(4,1)} %bitcast.113), calls=%async_computation.3 | async-start | bytes 8388608
  538.5 29.0 %slice-start.1 = ((s8[18350080]{0:T(1024)(128)(4,1)}), s8[4194304]{0:T(1024)(128)(4,1)S(1)}, s32[]{:S(2)}) async-start(s8[18350080]{0:T(1024)(128)(4,1)} %bitcast.113), calls=%async_computation.4 | async-start | bytes 8388608
  538.5 29.0 %slice-start.2 = ((s8[18350080]{0:T(1024)(128)(4,1)}), s8[4194304]{0:T(1024)(128)(4,1)S(1)}, s32[]{:S(2)}) async-start(s8[18350080]{0:T(1024)(128)(4,1)} %bitcast.113), calls=%async_computation.5 | async-start | bytes 8388608
  558.2 9.8 %slice-start.3 = ((s8[18350080]{0:T(1024)(128)(4,1)}), s8[4194304]{0:T(1024)(128)(4,1)S(1)}, s32[]{:S(2)}) async-start(s8[18350080]{0:T(1024)(128)(4,1)} %bitcast.113), calls=%async_computation.6 | async-start | bytes 8388608
  558.2 10.7 %slice-start.4 = ((s8[18350080]{0:T(1024)(128)(4,1)}), s8[1572864]{0:T(1024)(128)(4,1)S(1)}, s32[]{:S(2)}) async-start(s8[18350080]{0:T(1024)(128)(4,1)} %bitcast.113), calls=%async_computation.7 | async-start | bytes 3145728
Sparse Core Ops, SparseCore 0:
  261.3 90.7 all-gather.3
  354.5 90.7 all-gather.5
  447.7 90.7 all-gather.7

commit v2 on v1

v2 whole, which is shorter than its diff:
```python
import functools

import jax
import jax.numpy as jnp
from jax import lax
from jax.experimental import pallas as pl
from jax.experimental.pallas import tpu as pltpu
from jax.sharding import PartitionSpec as P

MESH = pl.DeviceIdType.MESH
DEVICES = 8
CHIPS = 4
LANES = 128
SPLIT = 4
SLOTS = 5
LANDING = 4
CHUNK = 112
PARTS = 2
HBM = pl.BlockSpec(memory_space=pl.ANY)
VMEM = pl.BlockSpec(memory_space=pltpu.VMEM)
DMA = pltpu.SemaphoreType.DMA


def tiled(a):
    *lead, rows, columns = a.shape
    a = a.reshape(*lead, rows // 8, 8, columns // LANES, LANES)
    return jnp.swapaxes(a, -3, -2).reshape(*lead, rows * columns // LANES, LANES)


def untiled(a, rows, columns):
    lead = a.shape[:-2]
    a = a.reshape(*lead, rows // 8, columns // LANES, 8, LANES)
    return jnp.swapaxes(a, -3, -2).reshape(*lead, rows, columns)


def place():
    me = lax.axis_index("dp")
    core = lax.rem(me, 2)
    x, y = me // 4, lax.rem(me // 2, 2)
    return me, core, x, y, me + 4 - 8 * x, me + 2 - 4 * y, me + 1 - 2 * core


def remote(src, dst, send, recv, to):
    return pltpu.make_async_remote_copy(src_ref=src, dst_ref=dst, send_sem=send, recv_sem=recv, device_id={"dp": to}, device_id_type=MESH)


def scatter_kernel(units, half, block, *refs):
    terms, weights, firsts, seconds = (refs[i : i + 3] for i in (0, 3, 6, 9))
    grad, held_w, held_m, held_v, total_ref = refs[12:17]
    own, part, sx, sy, sx2, sy2, rx, ry, rx2, ry2, acc, sums = refs[17:29]
    own_sem, part_send, part_recv, sx_sem, sy_sem, sx2_sem, sy2_sem = refs[29:36]
    rx_sem, ry_sem, rx2_sem, ry2_sem, state_sem, sum_send, sum_recv, credit, credit_x, credit_y = refs[36:]
    me, core, x, y, px, py, pc = place()
    here, beside_y, beside_x, across = 2 * x + y, 2 * x + 1 - y, 2 - 2 * x + y, 3 - 2 * x - y
    steps = half // CHUNK

    barrier = pltpu.get_barrier_semaphore()
    for k in range(1, DEVICES):
        pl.semaphore_signal(barrier, inc=1, device_id={"dp": lax.rem(me + k, DEVICES)}, device_id_type=MESH)
    pl.semaphore_wait(barrier, DEVICES - 1)

    def where(u):
        t = u // 3
        return lax.rem(u, 3), t // SPLIT, pl.multiple_of(lax.rem(t, SPLIT) * 2 * half, 16)

    def loads(u, term):
        _, layer, first = where(u)
        rows = pl.ds(first, 2 * half)
        slot = lax.rem(u, SLOTS)
        mine = pltpu.make_async_copy(term.at[layer, :, core, rows], own.at[slot], own_sem.at[slot])
        other = remote(term.at[layer, :, 1 - core, rows], part.at[slot], part_send.at[slot], part_recv.at[slot], pc)
        return mine, other

    def state():
        copies = []
        for k in range(3):
            mine = weights[k].at[:, pl.ds(pl.multiple_of(me * block, 16), block)]
            for n, (src, dst) in enumerate(((mine, held_w), (firsts[k], held_m), (seconds[k], held_v))):
                copies.append(pltpu.make_async_copy(src, dst.at[k], state_sem.at[3 * n + k]))
        return copies

    def prefetch(u):
        @pl.when(u >= SLOTS)
        def _():
            pl.semaphore_wait(credit, 1)

        for k in range(3):

            @pl.when(lax.rem(u, 3) == k)
            def _():
                for copy in loads(u, terms[k]):
                    copy.start()

    def first_x(u):
        two, land = lax.rem(u, 2), lax.rem(u, LANDING)
        return remote(sx.at[two], rx.at[land], sx_sem.at[two], rx_sem.at[land], px)

    def first_y(u):
        two, land = lax.rem(u, 2), lax.rem(u, LANDING)
        return remote(sy.at[two], ry.at[land], sy_sem.at[two], ry_sem.at[land], py)

    def second_x(u):
        two, land = lax.rem(u, 2), lax.rem(u, LANDING)
        return remote(sx2.at[two], rx2.at[land], sx2_sem.at[two], rx2_sem.at[land], px)

    def second_y(u):
        two, land = lax.rem(u, 2), lax.rem(u, LANDING)
        return remote(sy2.at[two], ry2.at[land], sy2_sem.at[two], ry2_sem.at[land], py)

    def pair(slot, chip, rows):
        return own[slot, chip, rows].astype(jnp.float32) + part[slot, chip, rows].astype(jnp.float32)

    def at(base, s):
        return pl.ds(pl.multiple_of(base + s * CHUNK, 16), CHUNK)

    def stage1(u):
        slot, two = lax.rem(u, SLOTS), lax.rem(u, 2)
        mine, other = loads(u, terms[0])
        mine.wait()
        other.wait()

        @pl.when(u >= 2)
        def _():
            first_x(u - 2).wait_send()
            first_y(u - 2).wait_send()

        def go(s, _):
            for n, chip in enumerate((beside_x, across)):
                sx[two, n, at(0, s)] = pair(slot, chip, at(0, s)).astype(jnp.bfloat16)
            for n, chip in enumerate((beside_y, across)):
                sy[two, n, at(0, s)] = pair(slot, chip, at(half, s)).astype(jnp.bfloat16)
            return 0

        lax.fori_loop(0, steps, go, 0)

        @pl.when(u >= LANDING)
        def _():
            pl.semaphore_wait(credit_x, 1)
            pl.semaphore_wait(credit_y, 1)

        first_x(u).start()
        first_y(u).start()

    def stage2(u):
        slot, two, land = lax.rem(u, SLOTS), lax.rem(u, 2), lax.rem(u, LANDING)
        first_x(u).wait_recv()
        first_y(u).wait_recv()

        @pl.when(u >= 2)
        def _():
            second_x(u - 2).wait_send()
            second_y(u - 2).wait_send()

        def go(s, _):
            r = at(0, s)
            sy2[two, r] = (pair(slot, beside_y, r) + rx[land, 1, r].astype(jnp.float32)).astype(jnp.bfloat16)
            sx2[two, r] = (pair(slot, beside_x, at(half, s)) + ry[land, 1, r].astype(jnp.float32)).astype(jnp.bfloat16)
            return 0

        lax.fori_loop(0, steps, go, 0)
        second_x(u).start()
        second_y(u).start()

    def stage3(u):
        slot, land = lax.rem(u, SLOTS), lax.rem(u, LANDING)
        weight, layer, first = where(u)
        second_x(u).wait_recv()
        second_y(u).wait_recv()

        def go(s, so_far):
            r = at(0, s)
            for base, near, far in ((0, rx, ry2), (half, ry, rx2)):
                g = pair(slot, here, at(base, s)) + near[land, 0, r].astype(jnp.float32) + far[land, r].astype(jnp.float32)
                g = g.astype(jnp.bfloat16)
                grad[weight, layer, at(first + base, s)] = g
                g = g.astype(jnp.float32)
                so_far = so_far + jnp.sum((g * g).reshape(CHUNK // 8, 8, LANES), axis=0)
            return so_far

        acc[...] += lax.fori_loop(0, steps, go, jnp.zeros((8, LANES), jnp.float32))

        @pl.when(u + SLOTS < units)
        def _():
            pl.semaphore_signal(credit, inc=1, device_id={"dp": pc}, device_id_type=MESH)

        @pl.when(u + LANDING < units)
        def _():
            pl.semaphore_signal(credit_x, inc=1, device_id={"dp": px}, device_id_type=MESH)
            pl.semaphore_signal(credit_y, inc=1, device_id={"dp": py}, device_id_type=MESH)

    acc[...] = jnp.zeros_like(acc)
    prefetch(0)
    prefetch(1)

    def body(i, _):
        @pl.when(i < units)
        def _():
            stage1(i)

        @pl.when(i + 2 < units)
        def _():
            prefetch(i + 2)

        @pl.when(i == 4)
        def _():
            for copy in state():
                copy.start()

        @pl.when(jnp.logical_and(i >= 1, i <= units))
        def _():
            stage2(i - 1)

        @pl.when(i >= 2)
        def _():
            stage3(i - 2)

        return 0

    lax.fori_loop(0, units + 2, body, 0)

    for k in range(1, DEVICES):
        remote(acc, sums.at[me], sum_send.at[k], sum_recv.at[me], lax.rem(me + k, DEVICES)).start()
    sums[me] = acc[...]
    for u in (units - 2, units - 1):
        for copy in (first_x(u), first_y(u), second_x(u), second_y(u)):
            copy.wait_send()
    for copy in state():
        copy.wait()
    for k in range(1, DEVICES):
        source = lax.rem(me + k, DEVICES)
        remote(acc, sums.at[source], sum_send.at[k], sum_recv.at[source], source).wait()
    total = sums[0]
    for d in range(1, DEVICES):
        total = total + sums[d]
    factor = jnp.minimum(1.0, 0.5 * lax.rsqrt(jnp.sum(total, keepdims=True) / (DEVICES * grad.size) + 1e-30))
    total_ref[...] = jnp.broadcast_to(factor, total_ref.shape)


def scatter(terms, weights, m, v):
    layers, block, _ = m[0].shape
    half = block // (2 * SPLIT)
    units = 3 * layers * SPLIT
    terms = [t.reshape(layers, CHIPS, 2, block, LANES) for t in terms]
    bf = functools.partial(pltpu.VMEM, dtype=jnp.bfloat16)
    return pl.pallas_call(
        functools.partial(scatter_kernel, units, half, block),
        out_shape=[
            pltpu.VMEM((3, layers, block, LANES), jnp.bfloat16),
            pltpu.VMEM((3, layers, block, LANES), jnp.bfloat16),
            pltpu.VMEM((3, layers, block, LANES), jnp.float32),
            pltpu.VMEM((3, layers, block, LANES), jnp.float32),
            pltpu.VMEM((8, LANES), jnp.float32),
        ],
        in_specs=[HBM] * 12,
        out_specs=[VMEM] * 5,
        scratch_shapes=[
            bf((SLOTS, CHIPS, 2 * half, LANES)),
            bf((SLOTS, CHIPS, 2 * half, LANES)),
            bf((2, 2, half, LANES)),
            bf((2, 2, half, LANES)),
            bf((2, half, LANES)),
            bf((2, half, LANES)),
            bf((LANDING, 2, half, LANES)),
            bf((LANDING, 2, half, LANES)),
            bf((LANDING, half, LANES)),
            bf((LANDING, half, LANES)),
            pltpu.VMEM((8, LANES), jnp.float32),
            pltpu.VMEM((DEVICES, 8, LANES), jnp.float32),
            DMA((SLOTS,)),
            DMA((SLOTS,)),
            DMA((SLOTS,)),
            DMA((2,)),
            DMA((2,)),
            DMA((2,)),
            DMA((2,)),
            DMA((LANDING,)),
            DMA((LANDING,)),
            DMA((LANDING,)),
            DMA((LANDING,)),
            DMA((9,)),
            DMA((DEVICES,)),
            DMA((DEVICES,)),
            pltpu.SemaphoreType.REGULAR,
            pltpu.SemaphoreType.REGULAR,
            pltpu.SemaphoreType.REGULAR,
        ],
        compiler_params=pltpu.CompilerParams(collective_id=0, has_side_effects=True, vmem_limit_bytes=17 << 20),
        name="scatter",
    )(*terms, *weights, *m, *v)


STEP_ROWS = 1120
STEP_CHUNK = 112
STEP_SLOTS = 3


def adam_kernel(layers, block, grad, held_w, held_m, held_v, factor_ref, *refs):
    firsts, seconds, new_w, stage_m, stage_v, stage_w, sem_m, sem_v, sem_w = refs[:3], refs[3:6], *refs[6:]
    factor = factor_ref[0:1, :]
    pieces = block // STEP_ROWS
    total = 3 * layers * pieces

    def stores(i, k):
        j, slot = i // 3, lax.rem(i, STEP_SLOTS)
        layer, rows = j // pieces, pl.ds(pl.multiple_of(lax.rem(j, pieces) * STEP_ROWS, 16), STEP_ROWS)
        return (
            pltpu.make_async_copy(stage_m.at[slot], firsts[k].at[layer, rows], sem_m.at[slot]),
            pltpu.make_async_copy(stage_v.at[slot], seconds[k].at[layer, rows], sem_v.at[slot]),
            pltpu.make_async_copy(stage_w.at[slot], new_w.at[k, layer, rows], sem_w.at[slot]),
        )

    def body(i, _):
        k, j, slot = lax.rem(i, 3), i // 3, lax.rem(i, STEP_SLOTS)
        layer, first = j // pieces, lax.rem(j, pieces) * STEP_ROWS

        @pl.when(i >= STEP_SLOTS)
        def _():
            for copy in stores(i - STEP_SLOTS, 0):
                copy.wait()

        def go(s, _):
            here = pl.ds(pl.multiple_of(s * STEP_CHUNK, 16), STEP_CHUNK)
            rows = pl.ds(pl.multiple_of(first + s * STEP_CHUNK, 16), STEP_CHUNK)
            g = grad[k, layer, rows].astype(jnp.float32) * factor
            w = held_w[k, layer, rows].astype(jnp.float32)
            m = 0.9 * held_m[k, layer, rows] + 0.1 * g
            v = 0.95 * held_v[k, layer, rows] + 0.05 * g * g
            stage_m[slot, here] = m
            stage_v[slot, here] = v
            stage_w[slot, here] = (w - 0.02 * (m * lax.rsqrt(v + 1e-8) + 0.1 * w)).astype(jnp.bfloat16)
            return 0

        lax.fori_loop(0, STEP_ROWS // STEP_CHUNK, go, 0)
        for n in range(3):

            @pl.when(k == n)
            def _():
                for copy in stores(i, n):
                    copy.start()

        return 0

    lax.fori_loop(0, total, body, 0)
    for i in range(total - STEP_SLOTS, total):
        for copy in stores(i, 0):
            copy.wait()


def adam(grad, held_w, held_m, held_v, factor):
    _, layers, block, _ = grad.shape
    moment = jax.ShapeDtypeStruct((layers, block, LANES), jnp.float32)
    *moments, new_w = pl.pallas_call(
        functools.partial(adam_kernel, layers, block),
        out_shape=[moment] * 6 + [pltpu.HBM((3, layers, block, LANES), jnp.bfloat16)],
        in_specs=[VMEM] * 5,
        out_specs=[HBM] * 7,
        scratch_shapes=[
            pltpu.VMEM((STEP_SLOTS, STEP_ROWS, LANES), jnp.float32),
            pltpu.VMEM((STEP_SLOTS, STEP_ROWS, LANES), jnp.float32),
            pltpu.VMEM((STEP_SLOTS, STEP_ROWS, LANES), jnp.bfloat16),
            DMA((STEP_SLOTS,)),
            DMA((STEP_SLOTS,)),
            DMA((STEP_SLOTS,)),
        ],
        compiler_params=pltpu.CompilerParams(vmem_limit_bytes=17 << 20),
        name="adam",
    )(*(pltpu.with_memory_space_constraint(a, pltpu.VMEM) for a in (grad, held_w, held_m, held_v, factor)))
    return moments, new_w


KINDS = 5


def gather_kernel(units, half, block, new_w, *refs):
    outs, (own_sem, x_send, x_recv, y_send, y_recv, x2_send, x2_recv, y2_send, y2_recv, c_send, c_recv) = refs[:3], refs[3:]
    me, core, x, y, px, py, pc = place()
    far = 7 - me - 1 + 2 * core
    barrier = pltpu.get_barrier_semaphore()
    for to in (px, py, pc):
        pl.semaphore_signal(barrier, inc=1, device_id={"dp": to}, device_id_type=MESH)
    pl.semaphore_wait(barrier, 3)

    def unit(u):
        t = u // 3
        return u % 3, t // PARTS, t % PARTS * 2 * half

    def rows(device, first, size):
        return pl.ds(pl.multiple_of(device * block + first, 16), size)

    def own(u):
        k, layer, first = unit(u)
        src = new_w.at[k, layer, pl.ds(first, 2 * half)]
        dst = outs[k].at[layer, rows(me, first, 2 * half)]
        return (
            remote(src, dst, x_send.at[u], x_recv.at[u], px),
            remote(src, dst, y_send.at[u], y_recv.at[u], py),
            remote(src, dst, c_send.at[u, 0], c_recv.at[u, 0], pc),
            pltpu.make_async_copy(src, dst, own_sem.at[u]),
        )

    def place_of(u, device, first, size):
        k, layer, base = unit(u)
        return outs[k].at[layer, rows(device, base + first, size)]

    def relay_y(u):
        ref = place_of(u, px, 0, half)
        return remote(ref, ref, y2_send.at[u], y2_recv.at[u], py)

    def relay_x(u):
        ref = place_of(u, py, half, half)
        return remote(ref, ref, x2_send.at[u], x2_recv.at[u], px)

    def across(u, kind, device, first, size):
        ref = place_of(u, device, first, size)
        return remote(ref, ref, c_send.at[u, kind], c_recv.at[u, kind], pc)

    def near(u):
        return across(u, 1, px, 0, 2 * half), across(u, 2, py, 0, 2 * half)

    def distant(u):
        return across(u, 3, far, 0, half), across(u, 4, far, half, half)

    for i in range(units + 2):
        if i < units:
            for copy in own(i):
                copy.start()
        if 1 <= i <= units:
            u = i - 1
            by_x, by_y, _, _ = own(u)
            by_x.wait_recv()
            by_y.wait_recv()
            for copy in (relay_x(u), relay_y(u), *near(u)):
                copy.start()
        if i >= 2:
            u = i - 2
            relay_x(u).wait_recv()
            relay_y(u).wait_recv()
            for copy in distant(u):
                copy.start()
    for u in range(units):
        by_x, by_y, by_c, local = own(u)
        by_x.wait_send()
        by_y.wait_send()
        by_c.wait()
        local.wait()
        relay_x(u).wait_send()
        relay_y(u).wait_send()
        for copy in (*near(u), *distant(u)):
            copy.wait()


def gather(new_w):
    _, layers, block, _ = new_w.shape
    units = 3 * layers * PARTS
    return pl.pallas_call(
        functools.partial(gather_kernel, units, block // (2 * PARTS), block),
        out_shape=[pltpu.VMEM((layers, DEVICES * block, LANES), jnp.bfloat16)] * 3,
        in_specs=[HBM],
        out_specs=[VMEM] * 3,
        scratch_shapes=[DMA((units,))] * 9 + [DMA((units, KINDS))] * 2,
        compiler_params=pltpu.CompilerParams(collective_id=1, has_side_effects=True, vmem_limit_bytes=1 << 20),
        name="gather",
    )(new_w)


def store_kernel(pieces, *refs):
    ins, outs, sem = refs[:3], refs[3:6], refs[6]
    layers, rows, _ = ins[0].shape
    size = rows // pieces
    copies = []
    for k in range(3):
        for layer in range(layers):
            for p in range(pieces):
                at = pl.ds(p * size, size)
                copies.append(pltpu.make_async_copy(ins[k].at[layer, at], outs[k].at[layer, at], sem.at[len(copies)]))
    for copy in copies:
        copy.start()
    for copy in copies:
        copy.wait()


def store(whole, pieces=2):
    shape = whole[0].shape
    return pl.pallas_call(
        functools.partial(store_kernel, pieces),
        out_shape=[jax.ShapeDtypeStruct(shape, jnp.bfloat16)] * 3,
        in_specs=[VMEM] * 3,
        out_specs=[HBM] * 3,
        scratch_shapes=[DMA((3 * shape[0] * pieces,))],
        compiler_params=pltpu.CompilerParams(vmem_limit_bytes=1 << 20),
        name="store",
    )(*(pltpu.with_memory_space_constraint(a, pltpu.VMEM) for a in whole))


def solution(mesh):
    def step(*arrays):
        shapes = [one.shape[1:] for one in arrays[3:6]]
        terms, weights, m, v = ([tiled(a) for a in arrays[i : i + 3]] for i in (0, 3, 6, 9))
        terms = [t[0] for t in terms]
        moments, new_w = adam(*scatter(terms, weights, m, v))
        whole = store(gather(new_w))
        whole = [untiled(w, *shape) for w, shape in zip(whole, shapes, strict=True)]
        moments = [untiled(one, shape[0] // DEVICES, shape[1]) for one, shape in zip(moments, shapes * 2, strict=True)]
        return (*whole, *moments)

    all_of, cut = P(None, None, None), P(None, "dp", None)
    return jax.shard_map(
        step,
        mesh=mesh,
        in_specs=(P(("rep", "dp"), None, None, None),) * 3 + (all_of,) * 3 + (cut,) * 6,
        out_specs=(P("rep", None, None),) * 3 + (P("rep", "dp", None),) * 6,
        check_vma=False,
    )
```

time: 582 us -> 493 us (0.85)
  Pallas kernels: 235 us -> 492 us
  waiting for transfers between devices: 254 us -> 0 us
  other arithmetic: 41.3 us -> 0 us
  local copies, waits for them, and re-layouts: 37.4 us -> 0 us
  between operations: 14.5 us -> 0.67 us
    pallas_call x1 -> x4, Pallas kernels: 235 us -> 492 us  [the longest x1 234 us: scatter(): pl.pallas_call(functools.partial(scatter_kernel, units, half, block), out...]
    all_gather x3 -> x0, waiting for transfers between devices: 254 us -> none  [step(): whole = [lax.all_gather(one[0], 'dp', axis=1, tiled=True) for one in new]]
    unnamed x21 -> x0, local copies, waits for them, and re-layouts: 37.4 us -> none
    convert_element_type x3 -> x0, other arithmetic: 21.3 us -> none  [adamw(): return ((w - 0.02 * step).astype(jnp.bfloat16), m, v)]
    mul x6 -> x0, other arithmetic: 18.7 us -> none  [the longest x3 10.4 us: adamw(): m = 0.9 * m + 0.1 * g]
  transfers between devices with their start and end apart: 3 -> 0, of which waited for: 3 -> 0; matrix products, arithmetic and copies ran while one was open for 4% -> 0% of each run, Pallas kernels for 0% -> 0%
where the time goes in v2:
time: 493 us
  Pallas kernels  492 us (100%)
    pallas_call x1, Pallas kernels, scatter(): pl.pallas_call(functools.partial(scatter_kernel, units, half, block), out...  234 us
    pallas_call x1, Pallas kernels, gather(): pl.pallas_call(functools.partial(gather_kernel, units, block // (2 * PART...  228 us
    pallas_call x1, Pallas kernels, store(): pl.pallas_call(functools.partial(store_kernel, pieces), out_shape=[jax.Sh...  17.6 us
    pallas_call x1, Pallas kernels, adam(): pl.pallas_call(functools.partial(adam_kernel, layers, block), out_shape=[...  12.9 us

profile of v2, /device:TPU:0, one launch (start us, length us, event | category | flops | bytes accessed | tf_op | source)
XLA Modules:
  0.0 492.9 jit_solution(8595598543711766976)
XLA Ops:
  0.6 234.1 %scatter.1 = (bf16[3,2,4480,128]{3,2,1,0:T(8,128)(2,1)S(1)}, bf16[3,2,4480,128]{3,2,1,0:T(8,128)(2,1)S(1)}, f32[3,2,4480,128]{3,2,1,0:T(8,128)S(1)}, f32[3,2,4480,128]{3,2,1,0:T(8,128)S(1)}, f32[8,128]{1,0:T(8,128)S(1)}) custom-call(bf16[2,4,2,4480,128]{4,3,2,1,0:T(8,128)(2,1)} %bitcast.105, bf16[2,4,2,4480,128]{4,3,2,1,0:T(8,128)(2,1)} %bitcast.106, ...), custom_call_target="tpu_custom_call" | custom-call | tf_op jit(solution)/shard_map/scatter/pallas_call | solution.py:245
  234.8 12.9 %adam.1 = (f32[2,4480,128]{2,1,0:T(8,128)}, f32[2,4480,128]{2,1,0:T(8,128)}, f32[2,4480,128]{2,1,0:T(8,128)}, f32[2,4480,128]{2,1,0:T(8,128)}, f32[2,4480,128]{2...) custom-call(bf16[3,2,4480,128]{3,2,1,0:T(8,128)(2,1)S(1)} %get-tuple-element.27.grad, ...), custom_call_target="tpu_custom_call" | custom-call | tf_op jit(solution)/shard_map/adam/pallas_call | solution.py:352
  247.7 227.7 %gather.1 = (bf16[2,35840,128]{2,1,0:T(8,128)(2,1)S(1)}, bf16[2,35840,128]{2,1,0:T(8,128)(2,1)S(1)}, bf16[2,35840,128]{2,1,0:T(8,128)(2,1)S(1)}) custom-call(bf16[3,2,4480,128]{3,2,1,0:T(8,128)(2,1)} %get-tuple-element.32.new_w), custom_call_target="tpu_custom_call" | custom-call | tf_op jit(solution)/shard_map/gather/pallas_call | solution.py:455
  475.4 17.6 %store.1 = (bf16[2,35840,128]{2,1,0:T(8,128)(2,1)}, bf16[2,35840,128]{2,1,0:T(8,128)(2,1)}, bf16[2,35840,128]{2,1,0:T(8,128)(2,1)}) custom-call(bf16[2,35840,128]{2,1,0:T(8,128)(2,1)S(1)} %get-tuple-element.33.refs_0_, bf16[2,35840,128]{2,1,0:T(8,128)(2,1)S(1)} %get-tuple-element.34.refs_1_, bf16[2,35840,128]{2,1,0:T(8,128)(2,1)S(1)} %get-tuple-element.35.refs_2_), custom_call_target="tpu_custom_call" | custom-call | tf_op jit(solution)/shard_map/store/pallas_call | solution.py:484

commit v3 on v2

--- a/solution.py
+++ b/solution.py
@@ -11,9 +11,11 @@
 DEVICES = 8
 CHIPS = 4
 LANES = 128
-SPLIT = 4
-SLOTS = 5
-LANDING = 4
+SPLIT = 10
+SLOTS = 8
+LANDING = 8
+LAG2 = 2
+LAG3 = 4
 CHUNK = 112
 PARTS = 2
 HBM = pl.BlockSpec(memory_space=pl.ANY)
@@ -206,17 +208,17 @@
             for copy in state():
                 copy.start()
 
-        @pl.when(jnp.logical_and(i >= 1, i <= units))
-        def _():
-            stage2(i - 1)
-
-        @pl.when(i >= 2)
-        def _():
-            stage3(i - 2)
+        @pl.when(jnp.logical_and(i >= LAG2, i < units + LAG2))
+        def _():
+            stage2(i - LAG2)
+
+        @pl.when(i >= LAG3)
+        def _():
+            stage3(i - LAG3)
 
         return 0
 
-    lax.fori_loop(0, units + 2, body, 0)
+    lax.fori_loop(0, units + LAG3, body, 0)
 
     for k in range(1, DEVICES):
         remote(acc, sums.at[me], sum_send.at[k], sum_recv.at[me], lax.rem(me + k, DEVICES)).start()
@@ -284,14 +286,52 @@
             pltpu.SemaphoreType.REGULAR,
             pltpu.SemaphoreType.REGULAR,
         ],
-        compiler_params=pltpu.CompilerParams(collective_id=0, has_side_effects=True, vmem_limit_bytes=17 << 20),
+        compiler_params=pltpu.CompilerParams(collective_id=0, has_side_effects=True, vmem_limit_bytes=VMEM_SHARED),
         name="scatter",
     )(*terms, *weights, *m, *v)
 
 
+VMEM_SHARED = 17 << 20
 STEP_ROWS = 1120
 STEP_CHUNK = 112
 STEP_SLOTS = 3
+ADAM_FLOPS = 1 << 34
+AHEAD = 1
+
+
+def adamw(grad, held_w, held_m, held_v, factor, at):
+    g = grad[at].astype(jnp.float32) * factor
+    w = held_w[at].astype(jnp.float32)
+    m = 0.9 * held_m[at] + 0.1 * g
+    v = 0.95 * held_v[at] + 0.05 * g * g
+    return m, v, w - 0.02 * (m * lax.rsqrt(v + 1e-8) + 0.1 * w)
+
+
+def ahead_kernel(grad, held_w, held_m, held_v, factor_ref, piece, stage, sem):
+    factor = factor_ref[0:1, :]
+    rows = stage.shape[0]
+
+    def go(s, _):
+        at = pl.ds(pl.multiple_of(s * STEP_CHUNK, 16), STEP_CHUNK)
+        stage[at] = adamw(grad, held_w, held_m, held_v, factor, (0, 0, at))[2].astype(jnp.bfloat16)
+        return 0
+
+    lax.fori_loop(0, rows // STEP_CHUNK, go, 0)
+    copy = pltpu.make_async_copy(stage, piece, sem)
+    copy.start()
+    copy.wait()
+
+
+def ahead(held, rows):
+    return pl.pallas_call(
+        ahead_kernel,
+        out_shape=pltpu.HBM((rows, LANES), jnp.bfloat16),
+        in_specs=[VMEM] * 5,
+        out_specs=HBM,
+        scratch_shapes=[pltpu.VMEM((rows, LANES), jnp.bfloat16), DMA],
+        compiler_params=pltpu.CompilerParams(vmem_limit_bytes=VMEM_SHARED),
+        name="ahead",
+    )(*(pltpu.with_memory_space_constraint(a, pltpu.VMEM) for a in held))
 
 
 def adam_kernel(layers, block, grad, held_w, held_m, held_v, factor_ref, *refs):
@@ -321,13 +361,10 @@
         def go(s, _):
             here = pl.ds(pl.multiple_of(s * STEP_CHUNK, 16), STEP_CHUNK)
             rows = pl.ds(pl.multiple_of(first + s * STEP_CHUNK, 16), STEP_CHUNK)
-            g = grad[k, layer, rows].astype(jnp.float32) * factor
-            w = held_w[k, layer, rows].astype(jnp.float32)
-            m = 0.9 * held_m[k, layer, rows] + 0.1 * g
-            v = 0.95 * held_v[k, layer, rows] + 0.05 * g * g
+            m, v, w = adamw(grad, held_w, held_m, held_v, factor, (k, layer, rows))
             stage_m[slot, here] = m
             stage_v[slot, here] = v
-            stage_w[slot, here] = (w - 0.02 * (m * lax.rsqrt(v + 1e-8) + 0.1 * w)).astype(jnp.bfloat16)
+            stage_w[slot, here] = w.astype(jnp.bfloat16)
             return 0
 
         lax.fori_loop(0, STEP_ROWS // STEP_CHUNK, go, 0)
@@ -362,7 +399,8 @@
             DMA((STEP_SLOTS,)),
             DMA((STEP_SLOTS,)),
         ],
-        compiler_params=pltpu.CompilerParams(vmem_limit_bytes=17 << 20),
+        compiler_params=pltpu.CompilerParams(vmem_limit_bytes=VMEM_SHARED),
+        cost_estimate=pl.CostEstimate(flops=ADAM_FLOPS, bytes_accessed=1 << 26, transcendentals=0),
         name="adam",
     )(*(pltpu.with_memory_space_constraint(a, pltpu.VMEM) for a in (grad, held_w, held_m, held_v, factor)))
     return moments, new_w
@@ -371,8 +409,8 @@
 KINDS = 5
 
 
-def gather_kernel(units, half, block, new_w, *refs):
-    outs, (own_sem, x_send, x_recv, y_send, y_recv, x2_send, x2_recv, y2_send, y2_recv, c_send, c_recv) = refs[:3], refs[3:]
+def gather_kernel(units, half, block, new_w, from_x, from_y, *refs):
+    outs, (own_sem, x_send, x_recv, y_send, y_recv, x2_send, x2_recv, y2_send, y2_recv, c_send, c_recv, early_sem) = refs[:3], refs[3:]
     me, core, x, y, px, py, pc = place()
     far = 7 - me - 1 + 2 * core
     barrier = pltpu.get_barrier_semaphore()
@@ -381,8 +419,8 @@
     pl.semaphore_wait(barrier, 3)
 
     def unit(u):
-        t = u // 3
-        return u % 3, t // PARTS, t % PARTS * 2 * half
+        k, t = divmod(u, units // 3)
+        return k, t // PARTS, t % PARTS * 2 * half
 
     def rows(device, first, size):
         return pl.ds(pl.multiple_of(device * block + first, 16), size)
@@ -402,45 +440,58 @@
         k, layer, base = unit(u)
         return outs[k].at[layer, rows(device, base + first, size)]
 
+    def early(u, device, first, size):
+        if u >= AHEAD:
+            return place_of(u, device, first, size)
+        return (from_x if device is px else from_y).at[pl.ds(u * 2 * half + first, size)]
+
     def relay_y(u):
-        ref = place_of(u, px, 0, half)
-        return remote(ref, ref, y2_send.at[u], y2_recv.at[u], py)
+        return remote(early(u, px, 0, half), place_of(u, px, 0, half), y2_send.at[u], y2_recv.at[u], py)
 
     def relay_x(u):
-        ref = place_of(u, py, half, half)
-        return remote(ref, ref, x2_send.at[u], x2_recv.at[u], px)
-
-    def across(u, kind, device, first, size):
+        return remote(early(u, py, half, half), place_of(u, py, half, half), x2_send.at[u], x2_recv.at[u], px)
+
+    def across(u, kind, device, first, size, src=None):
         ref = place_of(u, device, first, size)
-        return remote(ref, ref, c_send.at[u, kind], c_recv.at[u, kind], pc)
+        return remote(ref if src is None else src, ref, c_send.at[u, kind], c_recv.at[u, kind], pc)
 
     def near(u):
-        return across(u, 1, px, 0, 2 * half), across(u, 2, py, 0, 2 * half)
+        return tuple(across(u, n, device, 0, 2 * half, early(u, device, 0, 2 * half)) for n, device in ((1, px), (2, py)))
 
     def distant(u):
         return across(u, 3, far, 0, half), across(u, 4, far, half, half)
 
-    for i in range(units + 2):
+    def settle(u):
+        return tuple(pltpu.make_async_copy(early(u, device, 0, 2 * half), place_of(u, device, 0, 2 * half), early_sem.at[u, n]) for n, device in enumerate((px, py)))
+
+    for u in range(AHEAD):
+        for copy in (relay_x(u), relay_y(u), *near(u), *own(u)[2:], *settle(u)):
+            copy.start()
+    for i in range(AHEAD, units + 2):
         if i < units:
             for copy in own(i):
                 copy.start()
-        if 1 <= i <= units:
-            u = i - 1
+        u = i - 1
+        if AHEAD <= u < units:
             by_x, by_y, _, _ = own(u)
             by_x.wait_recv()
             by_y.wait_recv()
             for copy in (relay_x(u), relay_y(u), *near(u)):
                 copy.start()
-        if i >= 2:
-            u = i - 2
+        u = i - 2
+        if u >= 0:
             relay_x(u).wait_recv()
             relay_y(u).wait_recv()
             for copy in distant(u):
                 copy.start()
     for u in range(units):
         by_x, by_y, by_c, local = own(u)
-        by_x.wait_send()
-        by_y.wait_send()
+        if u >= AHEAD:
+            by_x.wait_send()
+            by_y.wait_send()
+        else:
+            for copy in settle(u):
+                copy.wait()
         by_c.wait()
         local.wait()
         relay_x(u).wait_send()
@@ -449,18 +500,18 @@
             copy.wait()
 
 
-def gather(new_w):
+def gather(new_w, from_x, from_y):
     _, layers, block, _ = new_w.shape
     units = 3 * layers * PARTS
     return pl.pallas_call(
         functools.partial(gather_kernel, units, block // (2 * PARTS), block),
         out_shape=[pltpu.VMEM((layers, DEVICES * block, LANES), jnp.bfloat16)] * 3,
-        in_specs=[HBM],
+        in_specs=[HBM] * 3,
         out_specs=[VMEM] * 3,
-        scratch_shapes=[DMA((units,))] * 9 + [DMA((units, KINDS))] * 2,
+        scratch_shapes=[DMA((units,))] * 9 + [DMA((units, KINDS))] * 2 + [DMA((max(AHEAD, 1), 2))],
         compiler_params=pltpu.CompilerParams(collective_id=1, has_side_effects=True, vmem_limit_bytes=1 << 20),
         name="gather",
-    )(new_w)
+    )(new_w, *(pltpu.with_memory_space_constraint(a, pltpu.HBM) for a in (from_x, from_y)))
 
 
 def store_kernel(pieces, *refs):
@@ -497,8 +548,11 @@
         shapes = [one.shape[1:] for one in arrays[3:6]]
         terms, weights, m, v = ([tiled(a) for a in arrays[i : i + 3]] for i in (0, 3, 6, 9))
         terms = [t[0] for t in terms]
-        moments, new_w = adam(*scatter(terms, weights, m, v))
-        whole = store(gather(new_w))
+        held = scatter(terms, weights, m, v)
+        piece = ahead(held, AHEAD * m[0].shape[1] // PARTS)
+        from_x, from_y = (lax.ppermute(piece, "dp", [(d, d ^ bit) for d in range(DEVICES)]) for bit in (4, 2))
+        moments, new_w = adam(*held)
+        whole = store(gather(new_w, from_x, from_y))
         whole = [untiled(w, *shape) for w, shape in zip(whole, shapes, strict=True)]
         moments = [untiled(one, shape[0] // DEVICES, shape[1]) for one, shape in zip(moments, shapes * 2, strict=True)]
         return (*whole, *moments)

time: 493 us -> 485 us (0.984)
  Pallas kernels: 492 us -> 480 us
    pallas_call x1, Pallas kernels: 228 us -> 215 us  [gather(): pl.pallas_call(functools.partial(gather_kernel, units, block // (2 * PART...]
  transfers between devices with their start and end apart: 0 -> 2, of which waited for: 0 -> 1; matrix products, arithmetic and copies ran while one was open for 0% -> 0% of each run, Pallas kernels for 0% -> 3%
where the time goes in v3:
time: 485 us
  Pallas kernels  480 us (99%)
    pallas_call x1, Pallas kernels, scatter(): pl.pallas_call(functools.partial(scatter_kernel, units, half, block), out...  233 us
    pallas_call x1, Pallas kernels, gather(): pl.pallas_call(functools.partial(gather_kernel, units, block // (2 * PART...  215 us
    pallas_call x1, Pallas kernels, store(): pl.pallas_call(functools.partial(store_kernel, pieces), out_shape=[jax.Sh...  17.6 us
    pallas_call x1, Pallas kernels, adam(): pl.pallas_call(functools.partial(adam_kernel, layers, block), out_shape=[...  12.8 us
  transfers between devices with their start and end apart: 2, of which 1 were waited for; matrix products, arithmetic and copies ran while one was open for 0% of the time, Pallas kernels for 3%

profile of v3, /device:TPU:0, one launch (start us, length us, event | category | flops | bytes accessed | tf_op | source)
XLA Modules:
  0.0 484.8 jit_solution(6066801071707346918)
XLA Ops:
  0.6 233.3 %scatter.1 = (bf16[3,2,4480,128]{3,2,1,0:T(8,128)(2,1)S(1)}, bf16[3,2,4480,128]{3,2,1,0:T(8,128)(2,1)S(1)}, f32[3,2,4480,128]{3,2,1,0:T(8,128)S(1)}, f32[3,2,4480,128]{3,2,1,0:T(8,128)S(1)}, f32[8,128]{1,0:T(8,128)S(1)}) custom-call(bf16[2,4,2,4480,128]{4,3,2,1,0:T(8,128)(2,1)} %bitcast.105, bf16[2,4,2,4480,128]{4,3,2,1,0:T(8,128)(2,1)} %bitcast.106, ...), custom_call_target="tpu_custom_call" | custom-call | tf_op jit(solution)/shard_map/scatter/pallas_call | solution.py:247
  233.9 1.7 ahead.1
  235.6 1.3 collective-permute-start.1
  236.9 0.9 collective-permute-start
  237.8 12.8 %adam.1 = (f32[2,4480,128]{2,1,0:T(8,128)}, f32[2,4480,128]{2,1,0:T(8,128)}, f32[2,4480,128]{2,1,0:T(8,128)}, f32[2,4480,128]{2,1,0:T(8,128)}, f32[2,4480,128]{2...) custom-call(bf16[3,2,4480,128]{3,2,1,0:T(8,128)(2,1)S(1)} %get-tuple-element.27.grad, ...), custom_call_target="tpu_custom_call" | custom-call | flops 17179869184 | bytes 67108864 | tf_op jit(solution)/shard_map/adam/pallas_call | solution.py:389
  250.6 0.0 collective-permute-done.1.from_y
  250.6 0.0 copy-start
  250.7 1.0 collective-permute-done.from_x
  251.6 0.0 copy-start.1
  251.6 0.0 copy-done
  251.6 0.8 copy-done.1
  252.4 214.8 %gather.1 = (bf16[2,35840,128]{2,1,0:T(8,128)(2,1)S(1)}, bf16[2,35840,128]{2,1,0:T(8,128)(2,1)S(1)}, bf16[2,35840,128]{2,1,0:T(8,128)(2,1)S(1)}) custom-call(bf16[3,2,4480,128]{3,2,1,0:T(8,128)(2,1)} %get-tuple-element.32.new_w, bf16[2240,128]{1,0:T(8,128)(2,1)} %copy-done.1, bf16[2240,128]{1,0:T(8,128)(2,1)} %copy-done), custom_call_target="tpu_custom_call" | custom-call | tf_op jit(solution)/shard_map/gather/pallas_call | solution.py:506
  467.3 17.6 %store.1 = (bf16[2,35840,128]{2,1,0:T(8,128)(2,1)}, bf16[2,35840,128]{2,1,0:T(8,128)(2,1)}, bf16[2,35840,128]{2,1,0:T(8,128)(2,1)}) custom-call(bf16[2,35840,128]{2,1,0:T(8,128)(2,1)S(1)} %get-tuple-element.33.refs_0_, bf16[2,35840,128]{2,1,0:T(8,128)(2,1)S(1)} %get-tuple-element.34.refs_1_, bf16[2,35840,128]{2,1,0:T(8,128)(2,1)S(1)} %get-tuple-element.35.refs_2_), custom_call_target="tpu_custom_call" | custom-call | tf_op jit(solution)/shard_map/store/pallas_call | solution.py:535
Async XLA Ops:
  235.6 15.0 %collective-permute-start.1 = (bf16[2240,128]{1,0:T(8,128)(2,1)}, bf16[2240,128]{1,0:T(8,128)(2,1)S(1)}, u32[]{:S(2)}, u32[]{:S(2)}) collective-permute-start(bf16[2240,128]{1,0:T(8,128)(2,1)} %ahead.1), channel_id=1, source_target_pairs={{0,2},{1,3},{2,0},{3,1},{4,6},{5,7},{6,4},{7,5}} | collective-permute-start | bytes 1720328 | tf_op jit(solution)/shard_map/ppermute | solution.py:553
  236.9 14.7 %collective-permute-start = (bf16[2240,128]{1,0:T(8,128)(2,1)}, bf16[2240,128]{1,0:T(8,128)(2,1)S(1)}, u32[]{:S(2)}, u32[]{:S(2)}) collective-permute-start(bf16[2240,128]{1,0:T(8,128)(2,1)} %ahead.1), channel_id=1, source_target_pairs={{0,4},{1,5},{2,6},{3,7},{4,0},{5,1},{6,2},{7,3}} | collective-permute-start | bytes 1720328 | tf_op jit(solution)/shard_map/ppermute | solution.py:553
  250.6 1.0 copy-start
  251.6 0.8 copy-start.1

commit v4 on v3

--- a/solution.py
+++ b/solution.py
@@ -17,7 +17,10 @@
 LAG2 = 2
 LAG3 = 4
 CHUNK = 112
-PARTS = 2
+UNIT = 4480
+FIRST = 2304
+LAST = 2752
+PIECE_CHUNK = 128
 HBM = pl.BlockSpec(memory_space=pl.ANY)
 VMEM = pl.BlockSpec(memory_space=pltpu.VMEM)
 DMA = pltpu.SemaphoreType.DMA
@@ -46,12 +49,20 @@
     return pltpu.make_async_remote_copy(src_ref=src, dst_ref=dst, send_sem=send, recv_sem=recv, device_id={"dp": to}, device_id_type=MESH)
 
 
+def adamw(grad, held_w, held_m, held_v, factor, at):
+    g = grad[at].astype(jnp.float32) * factor
+    w = held_w[at].astype(jnp.float32)
+    m = 0.9 * held_m[at] + 0.1 * g
+    v = 0.95 * held_v[at] + 0.05 * g * g
+    return m, v, w - 0.02 * (m * lax.rsqrt(v + 1e-8) + 0.1 * w)
+
+
 def scatter_kernel(units, half, block, *refs):
     terms, weights, firsts, seconds = (refs[i : i + 3] for i in (0, 3, 6, 9))
-    grad, held_w, held_m, held_v, total_ref = refs[12:17]
-    own, part, sx, sy, sx2, sy2, rx, ry, rx2, ry2, acc, sums = refs[17:29]
-    own_sem, part_send, part_recv, sx_sem, sy_sem, sx2_sem, sy2_sem = refs[29:36]
-    rx_sem, ry_sem, rx2_sem, ry2_sem, state_sem, sum_send, sum_recv, credit, credit_x, credit_y = refs[36:]
+    grad, held_w, held_m, held_v, total_ref, piece = refs[12:18]
+    own, part, sx, sy, sx2, sy2, rx, ry, rx2, ry2, acc, sums = refs[18:30]
+    own_sem, part_send, part_recv, sx_sem, sy_sem, sx2_sem, sy2_sem = refs[30:37]
+    rx_sem, ry_sem, rx2_sem, ry2_sem, state_sem, sum_send, sum_recv, credit, credit_x, credit_y = refs[37:]
     me, core, x, y, px, py, pc = place()
     here, beside_y, beside_x, across = 2 * x + y, 2 * x + 1 - y, 2 - 2 * x + y, 3 - 2 * x - y
     steps = half // CHUNK
@@ -236,6 +247,14 @@
         total = total + sums[d]
     factor = jnp.minimum(1.0, 0.5 * lax.rsqrt(jnp.sum(total, keepdims=True) / (DEVICES * grad.size) + 1e-30))
     total_ref[...] = jnp.broadcast_to(factor, total_ref.shape)
+    factor = jnp.broadcast_to(factor, (1, LANES))
+
+    def go(s, _):
+        rows = pl.ds(pl.multiple_of(s * PIECE_CHUNK, 16), PIECE_CHUNK)
+        piece[rows] = adamw(grad, held_w, held_m, held_v, factor, (0, 0, rows))[2].astype(jnp.bfloat16)
+        return 0
+
+    lax.fori_loop(0, piece.shape[0] // PIECE_CHUNK, go, 0)
 
 
 def scatter(terms, weights, m, v):
@@ -252,9 +271,10 @@
             pltpu.VMEM((3, layers, block, LANES), jnp.float32),
             pltpu.VMEM((3, layers, block, LANES), jnp.float32),
             pltpu.VMEM((8, LANES), jnp.float32),
+            pltpu.VMEM((FIRST, LANES), jnp.bfloat16),
         ],
         in_specs=[HBM] * 12,
-        out_specs=[VMEM] * 5,
+        out_specs=[VMEM] * 6,
         scratch_shapes=[
             bf((SLOTS, CHIPS, 2 * half, LANES)),
             bf((SLOTS, CHIPS, 2 * half, LANES)),
@@ -296,42 +316,6 @@
 STEP_CHUNK = 112
 STEP_SLOTS = 3
 ADAM_FLOPS = 1 << 34
-AHEAD = 1
-
-
-def adamw(grad, held_w, held_m, held_v, factor, at):
-    g = grad[at].astype(jnp.float32) * factor
-    w = held_w[at].astype(jnp.float32)
-    m = 0.9 * held_m[at] + 0.1 * g
-    v = 0.95 * held_v[at] + 0.05 * g * g
-    return m, v, w - 0.02 * (m * lax.rsqrt(v + 1e-8) + 0.1 * w)
-
-
-def ahead_kernel(grad, held_w, held_m, held_v, factor_ref, piece, stage, sem):
-    factor = factor_ref[0:1, :]
-    rows = stage.shape[0]
-
-    def go(s, _):
-        at = pl.ds(pl.multiple_of(s * STEP_CHUNK, 16), STEP_CHUNK)
-        stage[at] = adamw(grad, held_w, held_m, held_v, factor, (0, 0, at))[2].astype(jnp.bfloat16)
-        return 0
-
-    lax.fori_loop(0, rows // STEP_CHUNK, go, 0)
-    copy = pltpu.make_async_copy(stage, piece, sem)
-    copy.start()
-    copy.wait()
-
-
-def ahead(held, rows):
-    return pl.pallas_call(
-        ahead_kernel,
-        out_shape=pltpu.HBM((rows, LANES), jnp.bfloat16),
-        in_specs=[VMEM] * 5,
-        out_specs=HBM,
-        scratch_shapes=[pltpu.VMEM((rows, LANES), jnp.bfloat16), DMA],
-        compiler_params=pltpu.CompilerParams(vmem_limit_bytes=VMEM_SHARED),
-        name="ahead",
-    )(*(pltpu.with_memory_space_constraint(a, pltpu.VMEM) for a in held))
 
 
 def adam_kernel(layers, block, grad, held_w, held_m, held_v, factor_ref, *refs):
@@ -409,8 +393,22 @@
 KINDS = 5
 
 
-def gather_kernel(units, half, block, new_w, from_x, from_y, *refs):
-    outs, (own_sem, x_send, x_recv, y_send, y_recv, x2_send, x2_recv, y2_send, y2_recv, c_send, c_recv, early_sem) = refs[:3], refs[3:]
+def gather_units(layers, block):
+    units = [(0, 0, 0, FIRST), (0, 0, FIRST, block - FIRST)]
+    for k in range(3):
+        for layer in range(layers):
+            if (k, layer) not in ((0, 0), (2, layers - 1)):
+                units += [(k, layer, first, UNIT) for first in range(0, block, UNIT)]
+    return *units, (2, layers - 1, 0, block - LAST), (2, layers - 1, block - LAST, LAST)
+
+
+def gather_kernel(units, early, spare, new_w, from_x, from_y, *refs):
+    count = 1 if spare is None else 3
+    outs, refs = refs[:count], refs[count:]
+    if spare is not None:
+        handed, refs = refs[0], refs[1:]
+        bounce, spare_sem, refs = refs[-2], refs[-1], refs[:-2]
+    own_sem, x_send, x_recv, y_send, y_recv, x2_send, x2_recv, y2_send, y2_recv, c_send, c_recv, early_sem = refs
     me, core, x, y, px, py, pc = place()
     far = 7 - me - 1 + 2 * core
     barrier = pltpu.get_barrier_semaphore()
@@ -418,129 +416,178 @@
         pl.semaphore_signal(barrier, inc=1, device_id={"dp": to}, device_id_type=MESH)
     pl.semaphore_wait(barrier, 3)
 
-    def unit(u):
-        k, t = divmod(u, units // 3)
-        return k, t // PARTS, t % PARTS * 2 * half
-
-    def rows(device, first, size):
-        return pl.ds(pl.multiple_of(device * block + first, 16), size)
-
-    def own(u):
-        k, layer, first = unit(u)
-        src = new_w.at[k, layer, pl.ds(first, 2 * half)]
-        dst = outs[k].at[layer, rows(me, first, 2 * half)]
+    def source(unit):
+        k, layer, first, rows = unit
+        return new_w.at[k, layer, pl.ds(first, rows)]
+
+    def place_of(n, device, half=None):
+        k, layer, first, rows = units[n]
+        ref = outs[0].at[device] if spare is None else outs[k].at[layer, device]
+        first = 0 if spare is None else first
+        return ref.at[pl.ds(first, rows) if half is None else pl.ds(first + half * rows // 2, rows // 2)]
+
+    def own(n):
+        src, dst = source(units[n]), place_of(n, me)
         return (
-            remote(src, dst, x_send.at[u], x_recv.at[u], px),
-            remote(src, dst, y_send.at[u], y_recv.at[u], py),
-            remote(src, dst, c_send.at[u, 0], c_recv.at[u, 0], pc),
-            pltpu.make_async_copy(src, dst, own_sem.at[u]),
+            remote(src, dst, x_send.at[n], x_recv.at[n], px),
+            remote(src, dst, y_send.at[n], y_recv.at[n], py),
+            remote(src, dst, c_send.at[n, 0], c_recv.at[n, 0], pc),
+            pltpu.make_async_copy(src, dst, own_sem.at[n]),
         )
 
-    def place_of(u, device, first, size):
-        k, layer, base = unit(u)
-        return outs[k].at[layer, rows(device, base + first, size)]
-
-    def early(u, device, first, size):
-        if u >= AHEAD:
-            return place_of(u, device, first, size)
-        return (from_x if device is px else from_y).at[pl.ds(u * 2 * half + first, size)]
-
-    def relay_y(u):
-        return remote(early(u, px, 0, half), place_of(u, px, 0, half), y2_send.at[u], y2_recv.at[u], py)
-
-    def relay_x(u):
-        return remote(early(u, py, half, half), place_of(u, py, half, half), x2_send.at[u], x2_recv.at[u], px)
-
-    def across(u, kind, device, first, size, src=None):
-        ref = place_of(u, device, first, size)
-        return remote(ref if src is None else src, ref, c_send.at[u, kind], c_recv.at[u, kind], pc)
-
-    def near(u):
-        return tuple(across(u, n, device, 0, 2 * half, early(u, device, 0, 2 * half)) for n, device in ((1, px), (2, py)))
-
-    def distant(u):
-        return across(u, 3, far, 0, half), across(u, 4, far, half, half)
-
-    def settle(u):
-        return tuple(pltpu.make_async_copy(early(u, device, 0, 2 * half), place_of(u, device, 0, 2 * half), early_sem.at[u, n]) for n, device in enumerate((px, py)))
-
-    for u in range(AHEAD):
-        for copy in (relay_x(u), relay_y(u), *near(u), *own(u)[2:], *settle(u)):
+    def landed(n, device, half=None):
+        if units[n] != early:
+            return place_of(n, device, half)
+        ref, rows = from_x if device is px else from_y, units[n][3]
+        return ref if half is None else ref.at[pl.ds(half * rows // 2, rows // 2)]
+
+    def relay_y(n):
+        return remote(landed(n, px, 0), place_of(n, px, 0), y2_send.at[n], y2_recv.at[n], py)
+
+    def relay_x(n):
+        return remote(landed(n, py, 1), place_of(n, py, 1), x2_send.at[n], x2_recv.at[n], px)
+
+    def across(n, kind, src, dst):
+        return remote(src, dst, c_send.at[n, kind], c_recv.at[n, kind], pc)
+
+    def near(n):
+        return tuple(across(n, kind, landed(n, device), place_of(n, device)) for kind, device in ((1, px), (2, py)))
+
+    def distant(n):
+        return tuple(across(n, 3 + half, place_of(n, far, half), place_of(n, far, half)) for half in (0, 1))
+
+    def settle(n):
+        if spare is None:
+            return ()
+        return tuple(pltpu.make_async_copy(landed(n, device), place_of(n, device), early_sem.at[k]) for k, device in enumerate((px, py)))
+
+    first = [n for n, unit in enumerate(units) if unit == early]
+    rest = [n for n, unit in enumerate(units) if unit != early]
+    for n in first:
+        for copy in (relay_x(n), relay_y(n), *near(n), *own(n)[2:], *settle(n)):
             copy.start()
-    for i in range(AHEAD, units + 2):
-        if i < units:
-            for copy in own(i):
+    for i in range(len(rest) + 1):
+        if i < len(rest):
+            for copy in own(rest[i]):
                 copy.start()
-        u = i - 1
-        if AHEAD <= u < units:
-            by_x, by_y, _, _ = own(u)
+        if spare is not None and i == 2:
+            copy = pltpu.make_async_copy(source(spare), bounce, spare_sem)
+            copy.start()
+            copy.wait()
+            pltpu.make_async_copy(bounce, handed, spare_sem).start()
+        if i >= 1:
+            n = rest[i - 1]
+            by_x, by_y, _, _ = own(n)
             by_x.wait_recv()
             by_y.wait_recv()
-            for copy in (relay_x(u), relay_y(u), *near(u)):
+            for copy in (relay_x(n), relay_y(n), *near(n)):
                 copy.start()
-        u = i - 2
-        if u >= 0:
-            relay_x(u).wait_recv()
-            relay_y(u).wait_recv()
-            for copy in distant(u):
+        done = first if i == 1 else [rest[i - 2]] if i >= 2 else []
+        for n in done if rest else first:
+            relay_x(n).wait_recv()
+            relay_y(n).wait_recv()
+            for copy in distant(n):
                 copy.start()
-    for u in range(units):
-        by_x, by_y, by_c, local = own(u)
-        if u >= AHEAD:
+    if rest:
+        relay_x(rest[-1]).wait_recv()
+        relay_y(rest[-1]).wait_recv()
+        for copy in distant(rest[-1]):
+            copy.start()
+    for n in range(len(units)):
+        by_x, by_y, by_c, local = own(n)
+        if n in rest:
             by_x.wait_send()
             by_y.wait_send()
-        else:
-            for copy in settle(u):
-                copy.wait()
+        for copy in settle(n) if n in first else ():
+            copy.wait()
         by_c.wait()
         local.wait()
-        relay_x(u).wait_send()
-        relay_y(u).wait_send()
-        for copy in (*near(u), *distant(u)):
+        relay_x(n).wait_send()
+        relay_y(n).wait_send()
+        for copy in (*near(n), *distant(n)):
             copy.wait()
-
-
-def gather(new_w, from_x, from_y):
+    if spare is not None:
+        pltpu.make_async_copy(bounce, handed, spare_sem).wait()
+
+
+def gather(new_w, from_x, from_y, units, early, spare=None):
     _, layers, block, _ = new_w.shape
-    units = 3 * layers * PARTS
+    n = len(units)
+    if spare is not None:
+        from_x, from_y = (pltpu.with_memory_space_constraint(a, pltpu.HBM) for a in (from_x, from_y))
+    if spare is None:
+        outs, specs, more = [pltpu.VMEM((DEVICES, early[3], LANES), jnp.bfloat16)], [VMEM], []
+    else:
+        piece = (spare[3], LANES)
+        outs = [pltpu.VMEM((layers, DEVICES, block, LANES), jnp.bfloat16)] * 3 + [pltpu.HBM(piece, jnp.bfloat16)]
+        specs, more = [VMEM] * 3 + [HBM], [pltpu.VMEM(piece, jnp.bfloat16), DMA]
     return pl.pallas_call(
-        functools.partial(gather_kernel, units, block // (2 * PARTS), block),
-        out_shape=[pltpu.VMEM((layers, DEVICES * block, LANES), jnp.bfloat16)] * 3,
+        functools.partial(gather_kernel, units, early, spare),
+        out_shape=outs,
         in_specs=[HBM] * 3,
-        out_specs=[VMEM] * 3,
-        scratch_shapes=[DMA((units,))] * 9 + [DMA((units, KINDS))] * 2 + [DMA((max(AHEAD, 1), 2))],
-        compiler_params=pltpu.CompilerParams(collective_id=1, has_side_effects=True, vmem_limit_bytes=1 << 20),
-        name="gather",
-    )(new_w, *(pltpu.with_memory_space_constraint(a, pltpu.HBM) for a in (from_x, from_y)))
-
-
-def store_kernel(pieces, *refs):
+        out_specs=specs,
+        scratch_shapes=[DMA((n,))] * 9 + [DMA((n, KINDS))] * 2 + [DMA((2,))] + more,
+        compiler_params=pltpu.CompilerParams(collective_id=1 if spare else 2, has_side_effects=True, vmem_limit_bytes=2 << 20),
+        name="gather" if spare else "gather_last",
+    )(pltpu.with_memory_space_constraint(new_w, pltpu.HBM), from_x, from_y)
+
+
+def store_kernel(*refs):
     ins, outs, sem = refs[:3], refs[3:6], refs[6]
-    layers, rows, _ = ins[0].shape
-    size = rows // pieces
+    layers, _, block, _ = ins[0].shape
     copies = []
-    for k in range(3):
-        for layer in range(layers):
-            for p in range(pieces):
-                at = pl.ds(p * size, size)
-                copies.append(pltpu.make_async_copy(ins[k].at[layer, at], outs[k].at[layer, at], sem.at[len(copies)]))
+    for k, layer in [(k, layer) for k in range(3) for layer in range(layers)]:
+        rows = pl.ds(0, block - LAST if (k, layer) == (2, layers - 1) else block)
+        copies.append(pltpu.make_async_copy(ins[k].at[layer, :, rows], outs[k].at[layer, :, rows], sem.at[len(copies)]))
     for copy in copies:
         copy.start()
     for copy in copies:
         copy.wait()
 
 
-def store(whole, pieces=2):
+def store(whole):
     shape = whole[0].shape
     return pl.pallas_call(
-        functools.partial(store_kernel, pieces),
+        store_kernel,
         out_shape=[jax.ShapeDtypeStruct(shape, jnp.bfloat16)] * 3,
         in_specs=[VMEM] * 3,
         out_specs=[HBM] * 3,
-        scratch_shapes=[DMA((3 * shape[0] * pieces,))],
-        compiler_params=pltpu.CompilerParams(vmem_limit_bytes=1 << 20),
+        scratch_shapes=[DMA((3 * shape[0],))],
+        compiler_params=pltpu.CompilerParams(vmem_limit_bytes=2 << 20),
+        cost_estimate=pl.CostEstimate(flops=ADAM_FLOPS, bytes_accessed=1 << 26, transcendentals=0),
         name="store",
     )(*(pltpu.with_memory_space_constraint(a, pltpu.VMEM) for a in whole))
+
+
+def store_last_kernel(last, from_x, from_y, _, out, sem):
+    layers, _, block, _ = out.shape
+    rows = last.shape[1]
+    copies = []
+    me = lax.axis_index("dp")
+    for bits in range(DEVICES):
+        device = me + sum((1 - 2 * lax.rem(me // bit, 2)) * bit for bit in (1, 2, 4) if bits & bit)
+        src = {4: from_x, 2: from_y}[bits] if bits in (4, 2) else last.at[device]
+        copies.append(pltpu.make_async_copy(src, out.at[layers - 1, device, pl.ds(block - rows, rows)], sem.at[len(copies)]))
+        copies[-1].start()
+    for copy in copies:
+        copy.wait()
+
+
+def store_last(last, from_x, from_y, stored):
+    return pl.pallas_call(
+        store_last_kernel,
+        out_shape=jax.ShapeDtypeStruct(stored.shape, stored.dtype),
+        in_specs=[VMEM] + [HBM] * 3,
+        out_specs=HBM,
+        scratch_shapes=[DMA((DEVICES,))],
+        input_output_aliases={3: 0},
+        compiler_params=pltpu.CompilerParams(vmem_limit_bytes=2 << 20),
+        name="store_last",
+    )(pltpu.with_memory_space_constraint(last, pltpu.VMEM), from_x, from_y, stored)
+
+
+def beside(piece):
+    return tuple(lax.ppermute(piece, "dp", [(d, d ^ bit) for d in range(DEVICES)]) for bit in (4, 2))
 
 
 def solution(mesh):
@@ -548,12 +595,17 @@
         shapes = [one.shape[1:] for one in arrays[3:6]]
         terms, weights, m, v = ([tiled(a) for a in arrays[i : i + 3]] for i in (0, 3, 6, 9))
         terms = [t[0] for t in terms]
-        held = scatter(terms, weights, m, v)
-        piece = ahead(held, AHEAD * m[0].shape[1] // PARTS)
-        from_x, from_y = (lax.ppermute(piece, "dp", [(d, d ^ bit) for d in range(DEVICES)]) for bit in (4, 2))
+        *held, piece = scatter(terms, weights, m, v)
+        layers, block, _ = m[0].shape
+        units = gather_units(layers, block)
+        near = beside(piece)
         moments, new_w = adam(*held)
-        whole = store(gather(new_w, from_x, from_y))
-        whole = [untiled(w, *shape) for w, shape in zip(whole, shapes, strict=True)]
+        *whole, piece = gather(new_w, *near, units[:-1], units[0], units[-1])
+        near_last = beside(piece)
+        whole = list(store(whole))
+        (last,) = gather(new_w, *near_last, units[-1:], units[-1])
+        whole[2] = store_last(last, *near_last, whole[2])
+        whole = [untiled(w.reshape(layers, -1, LANES), *shape) for w, shape in zip(whole, shapes, strict=True)]
         moments = [untiled(one, shape[0] // DEVICES, shape[1]) for one, shape in zip(moments, shapes * 2, strict=True)]
         return (*whole, *moments)
 

time: 485 us -> 476 us (0.981)
  Pallas kernels: 480 us -> 468 us
    pallas_call x3 -> x4, Pallas kernels: 234 us -> 221 us  [the longest x2 203 us: gather(): pl.pallas_call(functools.partial(gather_kernel, units, early, spare), out...]
  transfers between devices with their start and end apart: 2 -> 4, of which waited for: 1 -> 4; matrix products, arithmetic and copies ran while one was open for 0% -> 0% of each run, Pallas kernels for 3% -> 6%
where the time goes in v4:
time: 476 us
  Pallas kernels  468 us (98%)
    pallas_call x1, Pallas kernels, scatter(): pl.pallas_call(functools.partial(scatter_kernel, units, half, block), out...  234 us
    pallas_call x2, Pallas kernels, gather(): pl.pallas_call(functools.partial(gather_kernel, units, early, spare), out...  203 us
    pallas_call x1, Pallas kernels, store(): pl.pallas_call(store_kernel, out_shape=[jax.ShapeDtypeStruct(shape, jnp.b...  15.9 us
    pallas_call x1, Pallas kernels, adam(): pl.pallas_call(functools.partial(adam_kernel, layers, block), out_shape=[...  12.9 us
  transfers between devices with their start and end apart: 4, of which 4 were waited for; matrix products, arithmetic and copies ran while one was open for 0% of the time, Pallas kernels for 6%

profile of v4, /device:TPU:0, one launch (start us, length us, event | category | flops | bytes accessed | tf_op | source)
XLA Modules:
  0.0 476.1 jit_solution(13838880107318632575)
XLA Ops:
  0.6 234.2 %scatter.1 = (bf16[3,2,4480,128]{3,2,1,0:T(8,128)(2,1)S(1)}, bf16[3,2,4480,128]{3,2,1,0:T(8,128)(2,1)S(1)}, f32[3,2,4480,128]{3,2,1,0:T(8,128)S(1)}, f32[3,2,448...) custom-call(bf16[2,4,2,4480,128]{4,3,2,1,0:T(8,128)(2,1)} %bitcast.106, ...), custom_call_target="tpu_custom_call" | custom-call | tf_op jit(solution)/shard_map/scatter/pallas_call | solution.py:266
  234.8 1.2 collective-permute-start
  236.0 1.0 collective-permute-start.1
  237.0 12.9 %adam.1 = (f32[2,4480,128]{2,1,0:T(8,128)}, f32[2,4480,128]{2,1,0:T(8,128)}, f32[2,4480,128]{2,1,0:T(8,128)}, f32[2,4480,128]{2,1,0:T(8,128)}, f32[2,4480,128]{2...) custom-call(bf16[3,2,4480,128]{3,2,1,0:T(8,128)(2,1)S(1)} %get-tuple-element.29.grad, ...), custom_call_target="tpu_custom_call" | custom-call | flops 17179869184 | bytes 67108864 | tf_op jit(solution)/shard_map/adam/pallas_call | solution.py:373
  249.9 0.3 collective-permute-done.from_x
  250.2 0.0 copy-start
  250.2 0.9 collective-permute-done.1.from_y
  251.1 0.0 copy-start.1
  251.1 0.0 copy-done
  251.1 0.8 copy-done.1
  251.9 190.9 %gather.1 = (bf16[2,8,4480,128]{3,2,1,0:T(8,128)(2,1)S(1)}, bf16[2,8,4480,128]{3,2,1,0:T(8,128)(2,1)S(1)}, bf16[2,8,4480,128]{3,2,1,0:T(8,128)(2,1)S(1)}, bf16[2752,128]{1,0:T(8,128)(2,1)}) custom-call(bf16[3,2,4480,128]{3,2,1,0:T(8,128)(2,1)} %get-tuple-element.34.new_w, bf16[2304,128]{1,0:T(8,128)(2,1)} %copy-done, bf16[2304,128]{1,0:T(8,128)(2,1)} %copy-done.1), custom_call_target="tpu_custom_call" | custom-call | tf_op jit(solution)/shard_map/gather/pallas_call | solution.py:524
  442.8 1.2 collective-permute-start.2
  444.0 0.9 collective-permute-start.3
  444.8 15.9 %store.1 = (bf16[2,8,4480,128]{3,2,1,0:T(8,128)(2,1)}, bf16[2,8,4480,128]{3,2,1,0:T(8,128)(2,1)}, bf16[2,8,4480,128]{3,2,1,0:T(8,128)(2,1)}) custom-call(bf16[2,8,4480,128]{3,2,1,0:T(8,128)(2,1)S(1)} %get-tuple-element.36.refs_0_, bf16[2,8,4480,128]{3,2,1,0:T(8,128)(2,1)S(1)} %get-tuple-element.37.refs_1_, ...), custom_call_target="tpu_custom_call" | custom-call | flops 17179869184 | bytes 67108864 | tf_op jit(solution)/shard_map/store/pallas_call | solution.py:550
  460.7 0.1 collective-permute-done.2.from_x
  460.9 0.9 collective-permute-done.3.from_y
  461.7 11.8 %gather_last.1.last = bf16[8,2752,128]{2,1,0:T(8,128)(2,1)S(1)} custom-call(bf16[3,2,4480,128]{3,2,1,0:T(8,128)(2,1)} %get-tuple-element.34.new_w, bf16[2752,128]{1,0:T(8,128)(2,1)S(1)} %collective-permute-done.2.from_x, bf16[2752,128]{1,0:T(8,128)(2,1)S(1)} %collective-permute-done.3.from_y), custom_call_target="tpu_custom_call" | custom-call | tf_op jit(solution)/shard_map/gather_last/pallas_call | solution.py:524
  473.5 2.5 store_last.1
Async XLA Ops:
  234.8 15.4 %collective-permute-start = (bf16[2304,128]{1,0:T(8,128)(2,1)S(1)}, bf16[2304,128]{1,0:T(8,128)(2,1)S(1)}, u32[]{:S(2)}, u32[]{:S(2)}) collective-permute-start(bf16[2304,128]{1,0:T(8,128)(2,1)S(1)} %get-tuple-element.35), channel_id=1, source_target_pairs={{0,4},{1,5},{2,6},{3,7},{4,0},{5,1},{6,2},{7,3}} | collective-permute-start | bytes 1769480 | tf_op jit(solution)/shard_map/ppermute | solution.py:590
  236.0 15.1 %collective-permute-start.1 = (bf16[2304,128]{1,0:T(8,128)(2,1)S(1)}, bf16[2304,128]{1,0:T(8,128)(2,1)S(1)}, u32[]{:S(2)}, u32[]{:S(2)}) collective-permute-start(bf16[2304,128]{1,0:T(8,128)(2,1)S(1)} %get-tuple-element.35), channel_id=1, source_target_pairs={{0,2},{1,3},{2,0},{3,1},{4,6},{5,7},{6,4},{7,5}} | collective-permute-start | bytes 1769480 | tf_op jit(solution)/shard_map/ppermute | solution.py:590
  250.2 0.9 copy-start
  251.1 0.8 copy-start.1
  442.8 18.1 %collective-permute-start.2 = (bf16[2752,128]{1,0:T(8,128)(2,1)}, bf16[2752,128]{1,0:T(8,128)(2,1)S(1)}, u32[]{:S(2)}, u32[]{:S(2)}) collective-permute-start(bf16[2752,128]{1,0:T(8,128)(2,1)} %get-tuple-element.41), channel_id=1, source_target_pairs={{0,4},{1,5},{2,6},{3,7},{4,0},{5,1},{6,2},{7,3}} | collective-permute-start | bytes 2113544 | tf_op jit(solution)/shard_map/ppermute | solution.py:590
  444.0 17.8 %collective-permute-start.3 = (bf16[2752,128]{1,0:T(8,128)(2,1)}, bf16[2752,128]{1,0:T(8,128)(2,1)S(1)}, u32[]{:S(2)}, u32[]{:S(2)}) collective-permute-start(bf16[2752,128]{1,0:T(8,128)(2,1)} %get-tuple-element.41), channel_id=1, source_target_pairs={{0,2},{1,3},{2,0},{3,1},{4,6},{5,7},{6,4},{7,5}} | collective-permute-start | bytes 2113544 | tf_op jit(solution)/shard_map/ppermute | solution.py:590

commit v5 on v4

--- a/solution.py
+++ b/solution.py
@@ -6,6 +6,7 @@
 from jax.experimental import pallas as pl
 from jax.experimental.pallas import tpu as pltpu
 from jax.sharding import PartitionSpec as P
+
 
 MESH = pl.DeviceIdType.MESH
 DEVICES = 8
@@ -18,8 +19,9 @@
 LAG3 = 4
 CHUNK = 112
 UNIT = 4480
-FIRST = 2304
-LAST = 2752
+FIRST = 2560
+LAST = 2656
+ENDING = 480
 PIECE_CHUNK = 128
 HBM = pl.BlockSpec(memory_space=pl.ANY)
 VMEM = pl.BlockSpec(memory_space=pltpu.VMEM)
@@ -43,6 +45,13 @@
     core = lax.rem(me, 2)
     x, y = me // 4, lax.rem(me // 2, 2)
     return me, core, x, y, me + 4 - 8 * x, me + 2 - 4 * y, me + 1 - 2 * core
+
+
+def greet(*devices):
+    barrier = pltpu.get_barrier_semaphore()
+    for to in devices:
+        pl.semaphore_signal(barrier, inc=1, device_id={"dp": to}, device_id_type=MESH)
+    pl.semaphore_wait(barrier, len(devices))
 
 
 def remote(src, dst, send, recv, to):
@@ -67,10 +76,7 @@
     here, beside_y, beside_x, across = 2 * x + y, 2 * x + 1 - y, 2 - 2 * x + y, 3 - 2 * x - y
     steps = half // CHUNK
 
-    barrier = pltpu.get_barrier_semaphore()
-    for k in range(1, DEVICES):
-        pl.semaphore_signal(barrier, inc=1, device_id={"dp": lax.rem(me + k, DEVICES)}, device_id_type=MESH)
-    pl.semaphore_wait(barrier, DEVICES - 1)
+    greet(px, py, pc)
 
     def where(u):
         t = u // 3
@@ -394,224 +400,254 @@
 
 
 def gather_units(layers, block):
-    units = [(0, 0, 0, FIRST), (0, 0, FIRST, block - FIRST)]
+    units = [(0, 0, FIRST, block - FIRST)]
     for k in range(3):
         for layer in range(layers):
             if (k, layer) not in ((0, 0), (2, layers - 1)):
                 units += [(k, layer, first, UNIT) for first in range(0, block, UNIT)]
-    return *units, (2, layers - 1, 0, block - LAST), (2, layers - 1, block - LAST, LAST)
-
-
-def gather_kernel(units, early, spare, new_w, from_x, from_y, *refs):
-    count = 1 if spare is None else 3
-    outs, refs = refs[:count], refs[count:]
-    if spare is not None:
-        handed, refs = refs[0], refs[1:]
-        bounce, spare_sem, refs = refs[-2], refs[-1], refs[:-2]
-    own_sem, x_send, x_recv, y_send, y_recv, x2_send, x2_recv, y2_send, y2_recv, c_send, c_recv, early_sem = refs
-    me, core, x, y, px, py, pc = place()
+    cut = block - LAST - ENDING
+    units += [(2, layers - 1, 0, cut), (2, layers - 1, cut, ENDING)]
+    return tuple(units), (0, 0, 0, FIRST), (2, layers - 1, block - LAST, LAST)
+
+
+def gather_kernel(units, permuted, new_w, *refs):
+    outs, handed, bounce, handed_sem, refs = refs[:3], refs[3], refs[4], refs[5], refs[6:]
+    own_sem, x_send, x_recv, y_send, y_recv, x2_send, x2_recv, y2_send, y2_recv, c_send, c_recv = refs
+    me, core, _, _, px, py, pc = place()
     far = 7 - me - 1 + 2 * core
-    barrier = pltpu.get_barrier_semaphore()
-    for to in (px, py, pc):
-        pl.semaphore_signal(barrier, inc=1, device_id={"dp": to}, device_id_type=MESH)
-    pl.semaphore_wait(barrier, 3)
+    greet(px, py, pc)
+    both = units + permuted
 
     def source(unit):
         k, layer, first, rows = unit
         return new_w.at[k, layer, pl.ds(first, rows)]
 
     def place_of(n, device, half=None):
-        k, layer, first, rows = units[n]
-        ref = outs[0].at[device] if spare is None else outs[k].at[layer, device]
-        first = 0 if spare is None else first
-        return ref.at[pl.ds(first, rows) if half is None else pl.ds(first + half * rows // 2, rows // 2)]
-
-    def own(n):
-        src, dst = source(units[n]), place_of(n, me)
-        return (
-            remote(src, dst, x_send.at[n], x_recv.at[n], px),
-            remote(src, dst, y_send.at[n], y_recv.at[n], py),
-            remote(src, dst, c_send.at[n, 0], c_recv.at[n, 0], pc),
-            pltpu.make_async_copy(src, dst, own_sem.at[n]),
-        )
-
-    def landed(n, device, half=None):
-        if units[n] != early:
-            return place_of(n, device, half)
-        ref, rows = from_x if device is px else from_y, units[n][3]
-        return ref if half is None else ref.at[pl.ds(half * rows // 2, rows // 2)]
-
-    def relay_y(n):
-        return remote(landed(n, px, 0), place_of(n, px, 0), y2_send.at[n], y2_recv.at[n], py)
-
-    def relay_x(n):
-        return remote(landed(n, py, 1), place_of(n, py, 1), x2_send.at[n], x2_recv.at[n], px)
-
-    def across(n, kind, src, dst):
-        return remote(src, dst, c_send.at[n, kind], c_recv.at[n, kind], pc)
+        k, layer, first, rows = both[n]
+        return outs[k].at[layer, device, pl.ds(first, rows) if half is None else pl.ds(first + half * rows // 2, rows // 2)]
+
+    def home(n):
+        src, dst = source(both[n]), place_of(n, me)
+        return remote(src, dst, c_send.at[n, 0], c_recv.at[n, 0], pc), pltpu.make_async_copy(src, dst, own_sem.at[n])
+
+    def abroad(n):
+        src, dst = source(both[n]), place_of(n, me)
+        return remote(src, dst, x_send.at[n], x_recv.at[n], px), remote(src, dst, y_send.at[n], y_recv.at[n], py)
+
+    def relays(n):
+        a, b = place_of(n, px, 0), place_of(n, py, 1)
+        return remote(b, b, x2_send.at[n], x2_recv.at[n], px), remote(a, a, y2_send.at[n], y2_recv.at[n], py)
+
+    def across(n, kind, ref):
+        return remote(ref, ref, c_send.at[n, kind], c_recv.at[n, kind], pc)
 
     def near(n):
-        return tuple(across(n, kind, landed(n, device), place_of(n, device)) for kind, device in ((1, px), (2, py)))
+        return across(n, 1, place_of(n, px)), across(n, 2, place_of(n, py))
 
     def distant(n):
-        return tuple(across(n, 3 + half, place_of(n, far, half), place_of(n, far, half)) for half in (0, 1))
-
-    def settle(n):
-        if spare is None:
-            return ()
-        return tuple(pltpu.make_async_copy(landed(n, device), place_of(n, device), early_sem.at[k]) for k, device in enumerate((px, py)))
-
-    first = [n for n, unit in enumerate(units) if unit == early]
-    rest = [n for n, unit in enumerate(units) if unit != early]
-    for n in first:
-        for copy in (relay_x(n), relay_y(n), *near(n), *own(n)[2:], *settle(n)):
+        return tuple(across(n, 3 + half, place_of(n, far, half)) for half in (0, 1))
+
+    def start(copies):
+        for copy in copies:
             copy.start()
-    for i in range(len(rest) + 1):
-        if i < len(rest):
-            for copy in own(rest[i]):
-                copy.start()
-        if spare is not None and i == 2:
-            copy = pltpu.make_async_copy(source(spare), bounce, spare_sem)
+
+    for i in range(len(units) + 1):
+        if i < len(units):
+            start((*abroad(i), *home(i)))
+        if i == 2:
+            copy = pltpu.make_async_copy(source(permuted[-1]), bounce, handed_sem)
             copy.start()
             copy.wait()
-            pltpu.make_async_copy(bounce, handed, spare_sem).start()
+            pltpu.make_async_copy(bounce, handed, handed_sem).start()
+            for n in range(len(units), len(both)):
+                start(home(n))
         if i >= 1:
-            n = rest[i - 1]
-            by_x, by_y, _, _ = own(n)
-            by_x.wait_recv()
-            by_y.wait_recv()
-            for copy in (relay_x(n), relay_y(n), *near(n)):
-                copy.start()
-        done = first if i == 1 else [rest[i - 2]] if i >= 2 else []
-        for n in done if rest else first:
-            relay_x(n).wait_recv()
-            relay_y(n).wait_recv()
-            for copy in distant(n):
-                copy.start()
-    if rest:
-        relay_x(rest[-1]).wait_recv()
-        relay_y(rest[-1]).wait_recv()
-        for copy in distant(rest[-1]):
-            copy.start()
+            for copy in abroad(i - 1):
+                copy.wait_recv()
+            start((*relays(i - 1), *near(i - 1)))
+        for n in [i - 2] * (i >= 2) + [i - 1] * (i == len(units)):
+            for copy in relays(n):
+                copy.wait_recv()
+            start(distant(n))
     for n in range(len(units)):
-        by_x, by_y, by_c, local = own(n)
-        if n in rest:
-            by_x.wait_send()
-            by_y.wait_send()
-        for copy in settle(n) if n in first else ():
-            copy.wait()
-        by_c.wait()
-        local.wait()
-        relay_x(n).wait_send()
-        relay_y(n).wait_send()
+        for copy in (*abroad(n), *relays(n)):
+            copy.wait_send()
         for copy in (*near(n), *distant(n)):
             copy.wait()
-    if spare is not None:
-        pltpu.make_async_copy(bounce, handed, spare_sem).wait()
-
-
-def gather(new_w, from_x, from_y, units, early, spare=None):
+    for n in range(len(both)):
+        for copy in home(n):
+            copy.wait()
+    pltpu.make_async_copy(bounce, handed, handed_sem).wait()
+
+
+def gather(new_w, units, permuted):
     _, layers, block, _ = new_w.shape
-    n = len(units)
-    if spare is not None:
-        from_x, from_y = (pltpu.with_memory_space_constraint(a, pltpu.HBM) for a in (from_x, from_y))
-    if spare is None:
-        outs, specs, more = [pltpu.VMEM((DEVICES, early[3], LANES), jnp.bfloat16)], [VMEM], []
-    else:
-        piece = (spare[3], LANES)
-        outs = [pltpu.VMEM((layers, DEVICES, block, LANES), jnp.bfloat16)] * 3 + [pltpu.HBM(piece, jnp.bfloat16)]
-        specs, more = [VMEM] * 3 + [HBM], [pltpu.VMEM(piece, jnp.bfloat16), DMA]
+    n = len(units) + len(permuted)
+    piece = (permuted[-1][3], LANES)
     return pl.pallas_call(
-        functools.partial(gather_kernel, units, early, spare),
+        functools.partial(gather_kernel, units, permuted),
+        out_shape=[pltpu.VMEM((layers, DEVICES, block, LANES), jnp.bfloat16)] * 3 + [pltpu.HBM(piece, jnp.bfloat16)],
+        in_specs=[HBM],
+        out_specs=[VMEM] * 3 + [HBM],
+        scratch_shapes=[pltpu.VMEM(piece, jnp.bfloat16), DMA] + [DMA((n,))] * 9 + [DMA((n, KINDS))] * 2,
+        compiler_params=pltpu.CompilerParams(collective_id=1, has_side_effects=True, vmem_limit_bytes=2 << 20),
+        name="gather",
+    )(pltpu.with_memory_space_constraint(new_w, pltpu.HBM))
+
+
+def relay_kernel(first_x, first_y, last_x, last_y, first, last, x_send, x_recv, y_send, y_recv, c_send, c_recv, settle_sem):
+    me, core, _, _, px, py, pc = place()
+    far = 7 - me - 1 + 2 * core
+    greet(px, py, pc)
+    end = last.shape[1] - ENDING
+    units = ((first, first_x, first_y, 0, first.shape[1]), (last, last_x, last_y, 0, end), (last, last_x, last_y, end, ENDING))
+
+    def halves(n):
+        _, _, _, base, rows = units[n]
+        return pl.ds(base, rows // 2), pl.ds(base + rows // 2, rows // 2)
+
+    def relays(n):
+        out, from_x, from_y, _, _ = units[n]
+        a, b = halves(n)
+        return (
+            remote(from_y.at[b], out.at[py, b], x_send.at[n], x_recv.at[n], px),
+            remote(from_x.at[a], out.at[px, a], y_send.at[n], y_recv.at[n], py),
+        )
+
+    def near():
+        return tuple(
+            remote(src, dst.at[device], c_send.at[k], c_recv.at[k], pc)
+            for k, (src, dst, device) in enumerate(((first_x, first, px), (first_y, first, py), (last_x, last, px), (last_y, last, py)))
+        )
+
+    def distant(n):
+        out = units[n][0]
+        copies = ((4 + 2 * n + half, out.at[far, rows]) for half, rows in enumerate(halves(n)))
+        return tuple(remote(ref, ref, c_send.at[k], c_recv.at[k], pc) for k, ref in copies)
+
+    settle = [pltpu.make_async_copy(src, first.at[device], settle_sem.at[k]) for k, (src, device) in enumerate(((first_x, px), (first_y, py)))]
+    for copy in (*relays(0), *relays(1), *relays(2), *near(), *settle):
+        copy.start()
+    for n in range(3):
+        for copy in relays(n):
+            copy.wait_recv()
+        for copy in distant(n):
+            copy.start()
+    for n in range(3):
+        for copy in relays(n):
+            copy.wait_send()
+        for copy in distant(n):
+            copy.wait()
+    for copy in (*near(), *settle):
+        copy.wait()
+
+
+def relay(near_first, near_last):
+    outs = [pltpu.VMEM((DEVICES, near[0].shape[0], LANES), jnp.bfloat16) for near in (near_first, near_last)]
+    return pl.pallas_call(
+        relay_kernel,
         out_shape=outs,
-        in_specs=[HBM] * 3,
-        out_specs=specs,
-        scratch_shapes=[DMA((n,))] * 9 + [DMA((n, KINDS))] * 2 + [DMA((2,))] + more,
-        compiler_params=pltpu.CompilerParams(collective_id=1 if spare else 2, has_side_effects=True, vmem_limit_bytes=2 << 20),
-        name="gather" if spare else "gather_last",
-    )(pltpu.with_memory_space_constraint(new_w, pltpu.HBM), from_x, from_y)
-
-
-def store_kernel(*refs):
-    ins, outs, sem = refs[:3], refs[3:6], refs[6]
-    layers, _, block, _ = ins[0].shape
-    copies = []
-    for k, layer in [(k, layer) for k in range(3) for layer in range(layers)]:
-        rows = pl.ds(0, block - LAST if (k, layer) == (2, layers - 1) else block)
-        copies.append(pltpu.make_async_copy(ins[k].at[layer, :, rows], outs[k].at[layer, :, rows], sem.at[len(copies)]))
+        in_specs=[HBM] * 4,
+        out_specs=[VMEM] * 2,
+        scratch_shapes=[DMA((3,))] * 4 + [DMA((10,))] * 2 + [DMA((2,))],
+        compiler_params=pltpu.CompilerParams(collective_id=2, has_side_effects=True, vmem_limit_bytes=2 << 20),
+        name="relay",
+    )(*(pltpu.with_memory_space_constraint(a, pltpu.HBM) for a in near_first), *near_last)
+
+
+def others():
+    me = lax.axis_index("dp")
+    for bits in range(2, DEVICES):
+        yield me + sum((1 - 2 * lax.rem(me // bit, 2)) * bit for bit in (1, 2, 4) if bits & bit), {4: 0, 2: 1}.get(bits)
+
+
+def copy_all(pairs, sem):
+    copies = [pltpu.make_async_copy(src, dst, sem.at[n]) for n, (src, dst) in enumerate(pairs)]
     for copy in copies:
         copy.start()
     for copy in copies:
         copy.wait()
 
 
-def store(whole):
+def store_kernel(permuted, *refs):
+    ins, outs, sem = refs[:3], refs[3:6], refs[6]
+    layers, _, block, _ = ins[0].shape
+    me = lax.axis_index("dp")
+    at = []
+    for k, layer in [(k, layer) for k in range(3) for layer in range(layers)]:
+        first, rows = next(((f, r) for one, two, f, r in permuted if (one, two) == (k, layer)), (block, 0))
+        at.append((k, (layer, pl.ds(0, DEVICES), pl.ds(0, first) if first else pl.ds(rows, block - rows))))
+        if rows:
+            at += [(k, (layer, device, pl.ds(first, rows))) for device in (me, me + 1 - 2 * lax.rem(me, 2))]
+    copy_all([(ins[k].at[where], outs[k].at[where]) for k, where in at], sem)
+
+
+def store(whole, permuted):
     shape = whole[0].shape
     return pl.pallas_call(
-        store_kernel,
+        functools.partial(store_kernel, permuted),
         out_shape=[jax.ShapeDtypeStruct(shape, jnp.bfloat16)] * 3,
         in_specs=[VMEM] * 3,
         out_specs=[HBM] * 3,
-        scratch_shapes=[DMA((3 * shape[0],))],
+        scratch_shapes=[DMA((3 * shape[0] + 4,))],
         compiler_params=pltpu.CompilerParams(vmem_limit_bytes=2 << 20),
         cost_estimate=pl.CostEstimate(flops=ADAM_FLOPS, bytes_accessed=1 << 26, transcendentals=0),
         name="store",
     )(*(pltpu.with_memory_space_constraint(a, pltpu.VMEM) for a in whole))
 
 
-def store_last_kernel(last, from_x, from_y, _, out, sem):
-    layers, _, block, _ = out.shape
-    rows = last.shape[1]
-    copies = []
-    me = lax.axis_index("dp")
-    for bits in range(DEVICES):
-        device = me + sum((1 - 2 * lax.rem(me // bit, 2)) * bit for bit in (1, 2, 4) if bits & bit)
-        src = {4: from_x, 2: from_y}[bits] if bits in (4, 2) else last.at[device]
-        copies.append(pltpu.make_async_copy(src, out.at[layers - 1, device, pl.ds(block - rows, rows)], sem.at[len(copies)]))
-        copies[-1].start()
-    for copy in copies:
-        copy.wait()
-
-
-def store_last(last, from_x, from_y, stored):
+def store_last_kernel(permuted, first, last, last_x, last_y, _, __, out_first, out_last, sem):
+    pairs = []
+    for device, beside in others():
+        for src, out, (_, layer, base, rows) in ((first, out_first, permuted[0]), (last, out_last, permuted[1])):
+            apart = src is last and beside is not None
+            pairs.append(((last_x, last_y)[beside] if apart else src.at[device], out.at[layer, device, pl.ds(base, rows)]))
+    copy_all(pairs, sem)
+
+
+def store_last(first, last, last_x, last_y, stored, permuted):
+    pieces = (pltpu.with_memory_space_constraint(a, pltpu.VMEM) for a in (first, last))
     return pl.pallas_call(
-        store_last_kernel,
-        out_shape=jax.ShapeDtypeStruct(stored.shape, stored.dtype),
-        in_specs=[VMEM] + [HBM] * 3,
-        out_specs=HBM,
-        scratch_shapes=[DMA((DEVICES,))],
-        input_output_aliases={3: 0},
+        functools.partial(store_last_kernel, permuted),
+        out_shape=[jax.ShapeDtypeStruct(a.shape, a.dtype) for a in stored],
+        in_specs=[VMEM] * 2 + [HBM] * 4,
+        out_specs=[HBM] * 2,
+        scratch_shapes=[DMA((2 * DEVICES,))],
+        input_output_aliases={4: 0, 5: 1},
         compiler_params=pltpu.CompilerParams(vmem_limit_bytes=2 << 20),
         name="store_last",
-    )(pltpu.with_memory_space_constraint(last, pltpu.VMEM), from_x, from_y, stored)
+    )(*pieces, last_x, last_y, *stored)
 
 
 def beside(piece):
-    return tuple(lax.ppermute(piece, "dp", [(d, d ^ bit) for d in range(DEVICES)]) for bit in (4, 2))
+    near = []
+    for bit in (4, 2):
+        near.append(lax.ppermute(piece, "dp", [(d, d ^ bit) for d in range(DEVICES)]))
+    return near
 
 
 def solution(mesh):
-    def step(*arrays):
+    def stages(*arrays):
         shapes = [one.shape[1:] for one in arrays[3:6]]
         terms, weights, m, v = ([tiled(a) for a in arrays[i : i + 3]] for i in (0, 3, 6, 9))
         terms = [t[0] for t in terms]
         *held, piece = scatter(terms, weights, m, v)
         layers, block, _ = m[0].shape
-        units = gather_units(layers, block)
-        near = beside(piece)
+        units, *permuted = gather_units(layers, block)
+        permuted = tuple(permuted)
+        near_first = beside(piece)
         moments, new_w = adam(*held)
-        *whole, piece = gather(new_w, *near, units[:-1], units[0], units[-1])
+        *whole, piece = gather(new_w, units, permuted)
         near_last = beside(piece)
-        whole = list(store(whole))
-        (last,) = gather(new_w, *near_last, units[-1:], units[-1])
-        whole[2] = store_last(last, *near_last, whole[2])
+        whole = list(store(whole, permuted))
+        whole[0], whole[2] = store_last(*relay(near_first, near_last), *near_last, whole[::2], permuted)
         whole = [untiled(w.reshape(layers, -1, LANES), *shape) for w, shape in zip(whole, shapes, strict=True)]
         moments = [untiled(one, shape[0] // DEVICES, shape[1]) for one, shape in zip(moments, shapes * 2, strict=True)]
         return (*whole, *moments)
 
     all_of, cut = P(None, None, None), P(None, "dp", None)
     return jax.shard_map(
-        step,
+        stages,
         mesh=mesh,
         in_specs=(P(("rep", "dp"), None, None, None),) * 3 + (all_of,) * 3 + (cut,) * 6,
         out_specs=(P("rep", None, None),) * 3 + (P("rep", "dp", None),) * 6,

time: 476 us -> 487 us (1.023)
  waiting for transfers between devices: 2.21 us -> 13.3 us
    ppermute x4, waiting for transfers between devices: 2.21 us -> 13.3 us  [beside(): lax.ppermute(piece, 'dp', [(d, d ^ bit) for d in range(DEVICES)])]
  transfers between devices with their start and end apart: 4 -> 4, of which waited for: 4 -> 2; matrix products, arithmetic and copies ran while one was open for 0% -> 0% of each run, Pallas kernels for 6% -> 3%
where the time goes in v5:
time: 487 us
  Pallas kernels  468 us (96%)
  waiting for transfers between devices  13.3 us (3%)
    pallas_call x1, Pallas kernels, scatter(): pl.pallas_call(functools.partial(scatter_kernel, units, half, block), out...  234 us
    pallas_call x1, Pallas kernels, gather(): pl.pallas_call(functools.partial(gather_kernel, units, permuted), out_sha...  184 us
    pallas_call x1, Pallas kernels, relay(): pl.pallas_call(relay_kernel, out_shape=outs, in_specs=[HBM] * 4, out_spec...  18.5 us
    pallas_call x1, Pallas kernels, store(): pl.pallas_call(functools.partial(store_kernel, permuted), out_shape=[jax....  15 us
    ppermute x4, waiting for transfers between devices, beside(): lax.ppermute(piece, 'dp', [(d, d ^ bit) for d in range(DEVICES)])  13.3 us
    pallas_call x1, Pallas kernels, adam(): pl.pallas_call(functools.partial(adam_kernel, layers, block), out_shape=[...  12.9 us
  transfers between devices with their start and end apart: 4, of which 2 were waited for; matrix products, arithmetic and copies ran while one was open for 0% of the time, Pallas kernels for 3%

profile of v5, /device:TPU:0, one launch (start us, length us, event | category | flops | bytes accessed | tf_op | source)
XLA Modules:
  0.0 486.6 jit_solution(5030438438843352683)
XLA Ops:
  0.6 234.1 %scatter.1 = (bf16[3,2,4480,128]{3,2,1,0:T(8,128)(2,1)S(1)}, bf16[3,2,4480,128]{3,2,1,0:T(8,128)(2,1)S(1)}, f32[3,2,4480,128]{3,2,1,0:T(8,128)S(1)}, f32[3,2,448...) custom-call(bf16[2,4,2,4480,128]{4,3,2,1,0:T(8,128)(2,1)} %bitcast.107, ...), custom_call_target="tpu_custom_call" | custom-call | tf_op jit(solution)/shard_map/scatter/pallas_call | solution.py:272
  234.8 12.9 %adam.1 = (f32[2,4480,128]{2,1,0:T(8,128)}, f32[2,4480,128]{2,1,0:T(8,128)}, f32[2,4480,128]{2,1,0:T(8,128)}, f32[2,4480,128]{2,1,0:T(8,128)}, f32[2,4480,128]{2...) custom-call(bf16[3,2,4480,128]{3,2,1,0:T(8,128)(2,1)S(1)} %get-tuple-element.34.grad, ...), custom_call_target="tpu_custom_call" | custom-call | flops 17179869184 | bytes 67108864 | tf_op jit(solution)/shard_map/adam/pallas_call | solution.py:379
  247.7 183.9 %gather.1 = (bf16[2,8,4480,128]{3,2,1,0:T(8,128)(2,1)S(1)}, bf16[2,8,4480,128]{3,2,1,0:T(8,128)(2,1)S(1)}, bf16[2,8,4480,128]{3,2,1,0:T(8,128)(2,1)S(1)}, bf16[2656,128]{1,0:T(8,128)(2,1)}) custom-call(bf16[3,2,4480,128]{3,2,1,0:T(8,128)(2,1)} %get-tuple-element.39.new_w), custom_call_target="tpu_custom_call" | custom-call | tf_op jit(solution)/shard_map/gather/pallas_call | solution.py:487
  431.6 0.9 collective-permute-start.2
  432.5 1.2 collective-permute-start.3
  433.6 0.9 collective-permute-start
  434.5 1.1 collective-permute-start.1
  435.7 15.0 %store.1 = (bf16[2,8,4480,128]{3,2,1,0:T(8,128)(2,1)}, bf16[2,8,4480,128]{3,2,1,0:T(8,128)(2,1)}, bf16[2,8,4480,128]{3,2,1,0:T(8,128)(2,1)}) custom-call(bf16[2,8,4480,128]{3,2,1,0:T(8,128)(2,1)S(1)} %get-tuple-element.43.refs_0_, bf16[2,8,4480,128]{3,2,1,0:T(8,128)(2,1)S(1)} %get-tuple-element.44.refs_1_, ...), custom_call_target="tpu_custom_call" | custom-call | flops 17179869184 | bytes 67108864 | tf_op jit(solution)/shard_map/store/pallas_call | solution.py:587
  450.7 12.7 %collective-permute-done.first_x = bf16[2560,128]{1,0:T(8,128)(2,1)S(1)} collective-permute-done((bf16[2560,128]{1,0:T(8,128)(2,1)S(1)}, bf16[2560,128]{1,0:T(8,128)(2,1)S(1)}, u32[]{:S(2)}, u32[]{:S(2)}) %collective-permute-start) | collective-permute-done | bytes 655392 | tf_op jit(solution)/shard_map/ppermute | solution.py:625
  463.4 0.0 copy-start
  463.4 0.6 collective-permute-done.1.first_y
  464.0 0.0 copy-start.1
  464.0 0.0 collective-permute-done.2.last_x
  464.0 0.0 collective-permute-done.3.last_y
  464.0 0.3 copy-done
  464.2 0.6 copy-done.1
  464.8 18.5 %relay.1 = (bf16[8,2560,128]{2,1,0:T(8,128)(2,1)S(1)}, bf16[8,2656,128]{2,1,0:T(8,128)(2,1)S(1)}) custom-call(bf16[2560,128]{1,0:T(8,128)(2,1)} %copy-done, bf16[2560,128]{1,0:T(8,128)(2,1)} %copy-done.1, bf16[2656,128]{1,0:T(8,128)(2,1)S(1)} %collective-permute-done.2.last_x, bf16[2656,128]{1,0:T(8,128)(2,1)S(1)} %collective-permute-done.3.last_y), custom_call_target="tpu_custom_call" | custom-call | tf_op jit(solution)/shard_map/relay/pallas_call | solution.py:547
  483.3 3.3 store_last.1
Async XLA Ops:
  431.6 32.4 %collective-permute-start.2 = (bf16[2656,128]{1,0:T(8,128)(2,1)}, bf16[2656,128]{1,0:T(8,128)(2,1)S(1)}, u32[]{:S(2)}, u32[]{:S(2)}) collective-permute-start(bf16[2656,128]{1,0:T(8,128)(2,1)} %get-tuple-element.40), channel_id=1, source_target_pairs={{0,4},{1,5},{2,6},{3,7},{4,0},{5,1},{6,2},{7,3}} | collective-permute-start | bytes 2039816 | tf_op jit(solution)/shard_map/ppermute | solution.py:625
  432.5 31.5 %collective-permute-start.3 = (bf16[2656,128]{1,0:T(8,128)(2,1)}, bf16[2656,128]{1,0:T(8,128)(2,1)S(1)}, u32[]{:S(2)}, u32[]{:S(2)}) collective-permute-start(bf16[2656,128]{1,0:T(8,128)(2,1)} %get-tuple-element.40), channel_id=1, source_target_pairs={{0,2},{1,3},{2,0},{3,1},{4,6},{5,7},{6,4},{7,5}} | collective-permute-start | bytes 2039816 | tf_op jit(solution)/shard_map/ppermute | solution.py:625
  433.6 29.7 %collective-permute-start = (bf16[2560,128]{1,0:T(8,128)(2,1)S(1)}, bf16[2560,128]{1,0:T(8,128)(2,1)S(1)}, u32[]{:S(2)}, u32[]{:S(2)}) collective-permute-start(bf16[2560,128]{1,0:T(8,128)(2,1)S(1)} %get-tuple-element.33), channel_id=1, source_target_pairs={{0,4},{1,5},{2,6},{3,7},{4,0},{5,1},{6,2},{7,3}} | collective-permute-start | bytes 1966088 | tf_op jit(solution)/shard_map/ppermute | solution.py:625
  434.5 29.5 %collective-permute-start.1 = (bf16[2560,128]{1,0:T(8,128)(2,1)S(1)}, bf16[2560,128]{1,0:T(8,128)(2,1)S(1)}, u32[]{:S(2)}, u32[]{:S(2)}) collective-permute-start(bf16[2560,128]{1,0:T(8,128)(2,1)S(1)} %get-tuple-element.33), channel_id=1, source_target_pairs={{0,2},{1,3},{2,0},{3,1},{4,6},{5,7},{6,4},{7,5}} | collective-permute-start | bytes 1966088 | tf_op jit(solution)/shard_map/ppermute | solution.py:625
  463.4 0.9 copy-start
  464.0 0.8 copy-start.1

commit v6 on v5

--- a/solution.py
+++ b/solution.py
@@ -19,10 +19,11 @@
 LAG3 = 4
 CHUNK = 112
 UNIT = 4480
-FIRST = 2560
-LAST = 2656
+FIRST = 2304
+LAST = 2528
+AHEAD = 2
 ENDING = 480
-PIECE_CHUNK = 128
+PIECE_CHUNK = 256
 HBM = pl.BlockSpec(memory_space=pl.ANY)
 VMEM = pl.BlockSpec(memory_space=pltpu.VMEM)
 DMA = pltpu.SemaphoreType.DMA
@@ -319,8 +320,8 @@
 
 VMEM_SHARED = 17 << 20
 STEP_ROWS = 1120
-STEP_CHUNK = 112
-STEP_SLOTS = 3
+STEP_CHUNK = 224
+STEP_SLOTS = 4
 ADAM_FLOPS = 1 << 34
 
 
@@ -411,7 +412,7 @@
 
 
 def gather_kernel(units, permuted, new_w, *refs):
-    outs, handed, bounce, handed_sem, refs = refs[:3], refs[3], refs[4], refs[5], refs[6:]
+    outs, handed, handed_sem, refs = refs[:3], refs[3], refs[4], refs[5:]
     own_sem, x_send, x_recv, y_send, y_recv, x2_send, x2_recv, y2_send, y2_recv, c_send, c_recv = refs
     me, core, _, _, px, py, pc = place()
     far = 7 - me - 1 + 2 * core
@@ -451,24 +452,22 @@
         for copy in copies:
             copy.start()
 
-    for i in range(len(units) + 1):
-        if i < len(units):
-            start((*abroad(i), *home(i)))
-        if i == 2:
-            copy = pltpu.make_async_copy(source(permuted[-1]), bounce, handed_sem)
-            copy.start()
-            copy.wait()
-            pltpu.make_async_copy(bounce, handed, handed_sem).start()
-            for n in range(len(units), len(both)):
-                start(home(n))
-        if i >= 1:
-            for copy in abroad(i - 1):
+    for n in range(AHEAD):
+        start((*abroad(n), *home(n)))
+    for n in range(len(units)):
+        if n + AHEAD < len(units):
+            start((*abroad(n + AHEAD), *home(n + AHEAD)))
+        if n == 2:
+            pltpu.make_async_copy(source(permuted[-1]), handed, handed_sem).start()
+            for k in range(len(units), len(both)):
+                start(home(k))
+        for copy in abroad(n):
+            copy.wait_recv()
+        start((*relays(n), *near(n)))
+        for k in [n - 1] * (n >= 1) + [n] * (n == len(units) - 1):
+            for copy in relays(k):
                 copy.wait_recv()
-            start((*relays(i - 1), *near(i - 1)))
-        for n in [i - 2] * (i >= 2) + [i - 1] * (i == len(units)):
-            for copy in relays(n):
-                copy.wait_recv()
-            start(distant(n))
+            start(distant(k))
     for n in range(len(units)):
         for copy in (*abroad(n), *relays(n)):
             copy.wait_send()
@@ -477,7 +476,7 @@
     for n in range(len(both)):
         for copy in home(n):
             copy.wait()
-    pltpu.make_async_copy(bounce, handed, handed_sem).wait()
+    pltpu.make_async_copy(source(permuted[-1]), handed, handed_sem).wait()
 
 
 def gather(new_w, units, permuted):
@@ -486,10 +485,10 @@
     piece = (permuted[-1][3], LANES)
     return pl.pallas_call(
         functools.partial(gather_kernel, units, permuted),
-        out_shape=[pltpu.VMEM((layers, DEVICES, block, LANES), jnp.bfloat16)] * 3 + [pltpu.HBM(piece, jnp.bfloat16)],
+        out_shape=[pltpu.VMEM((layers, DEVICES, block, LANES), jnp.bfloat16)] * 3 + [pltpu.VMEM(piece, jnp.bfloat16)],
         in_specs=[HBM],
-        out_specs=[VMEM] * 3 + [HBM],
-        scratch_shapes=[pltpu.VMEM(piece, jnp.bfloat16), DMA] + [DMA((n,))] * 9 + [DMA((n, KINDS))] * 2,
+        out_specs=[VMEM] * 4,
+        scratch_shapes=[DMA] + [DMA((n,))] * 9 + [DMA((n, KINDS))] * 2,
         compiler_params=pltpu.CompilerParams(collective_id=1, has_side_effects=True, vmem_limit_bytes=2 << 20),
         name="gather",
     )(pltpu.with_memory_space_constraint(new_w, pltpu.HBM))

time: 487 us -> 485 us (level)
  no operation moved by 1% of the time
where the time goes in v6:
time: 485 us
  Pallas kernels  468 us (96%)
  waiting for transfers between devices  10.8 us (2%)
    pallas_call x1, Pallas kernels, scatter(): pl.pallas_call(functools.partial(scatter_kernel, units, half, block), out...  234 us
    pallas_call x1, Pallas kernels, gather(): pl.pallas_call(functools.partial(gather_kernel, units, permuted), out_sha...  187 us
    pallas_call x1, Pallas kernels, relay(): pl.pallas_call(relay_kernel, out_shape=outs, in_specs=[HBM] * 4, out_spec...  17.4 us
    pallas_call x1, Pallas kernels, store(): pl.pallas_call(functools.partial(store_kernel, permuted), out_shape=[jax....  15.2 us
    pallas_call x1, Pallas kernels, adam(): pl.pallas_call(functools.partial(adam_kernel, layers, block), out_shape=[...  11.6 us
    ppermute x4, waiting for transfers between devices, beside(): lax.ppermute(piece, 'dp', [(d, d ^ bit) for d in range(DEVICES)])  10.8 us
  transfers between devices with their start and end apart: 4, of which 2 were waited for; matrix products, arithmetic and copies ran while one was open for 0% of the time, Pallas kernels for 3%

profile of v6, /device:TPU:0, one launch (start us, length us, event | category | flops | bytes accessed | tf_op | source)
XLA Modules:
  0.0 484.7 jit_solution(6492430754713170668)
XLA Ops:
  0.6 233.9 %scatter.1 = (bf16[3,2,4480,128]{3,2,1,0:T(8,128)(2,1)S(1)}, bf16[3,2,4480,128]{3,2,1,0:T(8,128)(2,1)S(1)}, f32[3,2,4480,128]{3,2,1,0:T(8,128)S(1)}, f32[3,2,448...) custom-call(bf16[2,4,2,4480,128]{4,3,2,1,0:T(8,128)(2,1)} %bitcast.107, ...), custom_call_target="tpu_custom_call" | custom-call | tf_op jit(solution)/shard_map/scatter/pallas_call | solution.py:273
  234.6 11.6 %adam.1 = (f32[2,4480,128]{2,1,0:T(8,128)}, f32[2,4480,128]{2,1,0:T(8,128)}, f32[2,4480,128]{2,1,0:T(8,128)}, f32[2,4480,128]{2,1,0:T(8,128)}, f32[2,4480,128]{2...) custom-call(bf16[3,2,4480,128]{3,2,1,0:T(8,128)(2,1)S(1)} %get-tuple-element.34.grad, ...), custom_call_target="tpu_custom_call" | custom-call | flops 17179869184 | bytes 67108864 | tf_op jit(solution)/shard_map/adam/pallas_call | solution.py:380
  246.2 187.1 %gather.1 = (bf16[2,8,4480,128]{3,2,1,0:T(8,128)(2,1)S(1)}, bf16[2,8,4480,128]{3,2,1,0:T(8,128)(2,1)S(1)}, bf16[2,8,4480,128]{3,2,1,0:T(8,128)(2,1)S(1)}, bf16[2528,128]{1,0:T(8,128)(2,1)S(1)}) custom-call(bf16[3,2,4480,128]{3,2,1,0:T(8,128)(2,1)} %get-tuple-element.39.new_w), custom_call_target="tpu_custom_call" | custom-call | tf_op jit(solution)/shard_map/gather/pallas_call | solution.py:486
  433.3 0.9 collective-permute-start.2
  434.2 1.2 collective-permute-start.3
  435.3 0.9 collective-permute-start
  436.2 1.1 collective-permute-start.1
  437.3 15.2 %store.1 = (bf16[2,8,4480,128]{3,2,1,0:T(8,128)(2,1)}, bf16[2,8,4480,128]{3,2,1,0:T(8,128)(2,1)}, bf16[2,8,4480,128]{3,2,1,0:T(8,128)(2,1)}) custom-call(bf16[2,8,4480,128]{3,2,1,0:T(8,128)(2,1)S(1)} %get-tuple-element.43.refs_0_, bf16[2,8,4480,128]{3,2,1,0:T(8,128)(2,1)S(1)} %get-tuple-element.44.refs_1_, ...), custom_call_target="tpu_custom_call" | custom-call | flops 17179869184 | bytes 67108864 | tf_op jit(solution)/shard_map/store/pallas_call | solution.py:586
  452.5 10.2 %collective-permute-done.first_x = bf16[2304,128]{1,0:T(8,128)(2,1)S(1)} collective-permute-done((bf16[2304,128]{1,0:T(8,128)(2,1)S(1)}, bf16[2304,128]{1,0:T(8,128)(2,1)S(1)}, u32[]{:S(2)}, u32[]{:S(2)}) %collective-permute-start) | collective-permute-done | bytes 589856 | tf_op jit(solution)/shard_map/ppermute | solution.py:624
  462.7 0.0 copy-start
  462.7 0.6 collective-permute-done.1.first_y
  463.3 0.0 copy-start.1
  463.3 0.0 collective-permute-done.2.last_x
  463.3 0.0 collective-permute-done.3.last_y
  463.4 0.2 copy-done
  463.6 0.6 copy-done.1
  464.2 17.4 %relay.1 = (bf16[8,2304,128]{2,1,0:T(8,128)(2,1)S(1)}, bf16[8,2528,128]{2,1,0:T(8,128)(2,1)S(1)}) custom-call(bf16[2304,128]{1,0:T(8,128)(2,1)} %copy-done, bf16[2304,128]{1,0:T(8,128)(2,1)} %copy-done.1, bf16[2528,128]{1,0:T(8,128)(2,1)S(1)} %collective-permute-done.2.last_x, bf16[2528,128]{1,0:T(8,128)(2,1)S(1)} %collective-permute-done.3.last_y), custom_call_target="tpu_custom_call" | custom-call | tf_op jit(solution)/shard_map/relay/pallas_call | solution.py:546
  481.5 3.2 store_last.1
Async XLA Ops:
  433.3 30.1 %collective-permute-start.2 = (bf16[2528,128]{1,0:T(8,128)(2,1)S(1)}, bf16[2528,128]{1,0:T(8,128)(2,1)S(1)}, u32[]{:S(2)}, u32[]{:S(2)}) collective-permute-start(bf16[2528,128]{1,0:T(8,128)(2,1)S(1)} %get-tuple-element.40), channel_id=1, source_target_pairs={{0,4},{1,5},{2,6},{3,7},{4,0},{5,1},{6,2},{7,3}} | collective-permute-start | bytes 1941512 | tf_op jit(solution)/shard_map/ppermute | solution.py:624
  434.2 29.2 %collective-permute-start.3 = (bf16[2528,128]{1,0:T(8,128)(2,1)S(1)}, bf16[2528,128]{1,0:T(8,128)(2,1)S(1)}, u32[]{:S(2)}, u32[]{:S(2)}) collective-permute-start(bf16[2528,128]{1,0:T(8,128)(2,1)S(1)} %get-tuple-element.40), channel_id=1, source_target_pairs={{0,2},{1,3},{2,0},{3,1},{4,6},{5,7},{6,4},{7,5}} | collective-permute-start | bytes 1941512 | tf_op jit(solution)/shard_map/ppermute | solution.py:624
  435.3 27.4 %collective-permute-start = (bf16[2304,128]{1,0:T(8,128)(2,1)S(1)}, bf16[2304,128]{1,0:T(8,128)(2,1)S(1)}, u32[]{:S(2)}, u32[]{:S(2)}) collective-permute-start(bf16[2304,128]{1,0:T(8,128)(2,1)S(1)} %get-tuple-element.33), channel_id=1, source_target_pairs={{0,4},{1,5},{2,6},{3,7},{4,0},{5,1},{6,2},{7,3}} | collective-permute-start | bytes 1769480 | tf_op jit(solution)/shard_map/ppermute | solution.py:624
  436.2 27.1 %collective-permute-start.1 = (bf16[2304,128]{1,0:T(8,128)(2,1)S(1)}, bf16[2304,128]{1,0:T(8,128)(2,1)S(1)}, u32[]{:S(2)}, u32[]{:S(2)}) collective-permute-start(bf16[2304,128]{1,0:T(8,128)(2,1)S(1)} %get-tuple-element.33), channel_id=1, source_target_pairs={{0,2},{1,3},{2,0},{3,1},{4,6},{5,7},{6,4},{7,5}} | collective-permute-start | bytes 1769480 | tf_op jit(solution)/shard_map/ppermute | solution.py:624
  462.7 0.8 copy-start
  463.3 0.8 copy-start.1

commit v7 on v6

--- a/solution.py
+++ b/solution.py
@@ -18,7 +18,6 @@
 LAG2 = 2
 LAG3 = 4
 CHUNK = 112
-UNIT = 4480
 FIRST = 2304
 LAST = 2528
 AHEAD = 2
@@ -402,10 +401,9 @@
 
 def gather_units(layers, block):
     units = [(0, 0, FIRST, block - FIRST)]
-    for k in range(3):
-        for layer in range(layers):
-            if (k, layer) not in ((0, 0), (2, layers - 1)):
-                units += [(k, layer, first, UNIT) for first in range(0, block, UNIT)]
+    units += [(0, layer, 0, block) for layer in range(1, layers)]
+    units.append((1, None, 0, block))
+    units += [(2, layer, 0, block) for layer in range(layers - 1)]
     cut = block - LAST - ENDING
     units += [(2, layers - 1, 0, cut), (2, layers - 1, cut, ENDING)]
     return tuple(units), (0, 0, 0, FIRST), (2, layers - 1, block - LAST, LAST)
@@ -419,13 +417,16 @@
     greet(px, py, pc)
     both = units + permuted
 
+    def layers_of(layer):
+        return pl.ds(0, outs[0].shape[0]) if layer is None else layer
+
     def source(unit):
         k, layer, first, rows = unit
-        return new_w.at[k, layer, pl.ds(first, rows)]
+        return new_w.at[k, layers_of(layer), pl.ds(first, rows)]
 
     def place_of(n, device, half=None):
         k, layer, first, rows = both[n]
-        return outs[k].at[layer, device, pl.ds(first, rows) if half is None else pl.ds(first + half * rows // 2, rows // 2)]
+        return outs[k].at[layers_of(layer), device, pl.ds(first, rows) if half is None else pl.ds(first + half * rows // 2, rows // 2)]
 
     def home(n):
         src, dst = source(both[n]), place_of(n, me)

time: 485 us -> 485 us (level)
  no operation moved by 1% of the time
where the time goes in v7:
time: 485 us
  Pallas kernels  468 us (96%)
  waiting for transfers between devices  10.8 us (2%)
    pallas_call x1, Pallas kernels, scatter(): pl.pallas_call(functools.partial(scatter_kernel, units, half, block), out...  234 us
    pallas_call x1, Pallas kernels, gather(): pl.pallas_call(functools.partial(gather_kernel, units, permuted), out_sha...  187 us
    pallas_call x1, Pallas kernels, relay(): pl.pallas_call(relay_kernel, out_shape=outs, in_specs=[HBM] * 4, out_spec...  17.4 us
    pallas_call x1, Pallas kernels, store(): pl.pallas_call(functools.partial(store_kernel, permuted), out_shape=[jax....  15.2 us
    pallas_call x1, Pallas kernels, adam(): pl.pallas_call(functools.partial(adam_kernel, layers, block), out_shape=[...  11.6 us
    ppermute x4, waiting for transfers between devices, beside(): lax.ppermute(piece, 'dp', [(d, d ^ bit) for d in range(DEVICES)])  10.8 us
  transfers between devices with their start and end apart: 4, of which 2 were waited for; matrix products, arithmetic and copies ran while one was open for 0% of the time, Pallas kernels for 3%

profile of v7, /device:TPU:0, one launch (start us, length us, event | category | flops | bytes accessed | tf_op | source)
XLA Modules:
  0.0 484.5 jit_solution(17977248805799776844)
XLA Ops:
  0.6 233.9 %scatter.1 = (bf16[3,2,4480,128]{3,2,1,0:T(8,128)(2,1)S(1)}, bf16[3,2,4480,128]{3,2,1,0:T(8,128)(2,1)S(1)}, f32[3,2,4480,128]{3,2,1,0:T(8,128)S(1)}, f32[3,2,448...) custom-call(bf16[2,4,2,4480,128]{4,3,2,1,0:T(8,128)(2,1)} %bitcast.107, ...), custom_call_target="tpu_custom_call" | custom-call | tf_op jit(solution)/shard_map/scatter/pallas_call | solution.py:272
  234.6 11.6 %adam.1 = (f32[2,4480,128]{2,1,0:T(8,128)}, f32[2,4480,128]{2,1,0:T(8,128)}, f32[2,4480,128]{2,1,0:T(8,128)}, f32[2,4480,128]{2,1,0:T(8,128)}, f32[2,4480,128]{2...) custom-call(bf16[3,2,4480,128]{3,2,1,0:T(8,128)(2,1)S(1)} %get-tuple-element.34.grad, ...), custom_call_target="tpu_custom_call" | custom-call | flops 17179869184 | bytes 67108864 | tf_op jit(solution)/shard_map/adam/pallas_call | solution.py:379
  246.2 186.9 %gather.1 = (bf16[2,8,4480,128]{3,2,1,0:T(8,128)(2,1)S(1)}, bf16[2,8,4480,128]{3,2,1,0:T(8,128)(2,1)S(1)}, bf16[2,8,4480,128]{3,2,1,0:T(8,128)(2,1)S(1)}, bf16[2528,128]{1,0:T(8,128)(2,1)S(1)}) custom-call(bf16[3,2,4480,128]{3,2,1,0:T(8,128)(2,1)} %get-tuple-element.39.new_w), custom_call_target="tpu_custom_call" | custom-call | tf_op jit(solution)/shard_map/gather/pallas_call | solution.py:487
  433.1 0.9 collective-permute-start.2
  434.0 1.2 collective-permute-start.3
  435.1 0.9 collective-permute-start
  436.0 1.1 collective-permute-start.1
  437.2 15.2 %store.1 = (bf16[2,8,4480,128]{3,2,1,0:T(8,128)(2,1)}, bf16[2,8,4480,128]{3,2,1,0:T(8,128)(2,1)}, bf16[2,8,4480,128]{3,2,1,0:T(8,128)(2,1)}) custom-call(bf16[2,8,4480,128]{3,2,1,0:T(8,128)(2,1)S(1)} %get-tuple-element.43.refs_0_, bf16[2,8,4480,128]{3,2,1,0:T(8,128)(2,1)S(1)} %get-tuple-element.44.refs_1_, ...), custom_call_target="tpu_custom_call" | custom-call | flops 17179869184 | bytes 67108864 | tf_op jit(solution)/shard_map/store/pallas_call | solution.py:587
  452.3 10.2 %collective-permute-done.first_x = bf16[2304,128]{1,0:T(8,128)(2,1)S(1)} collective-permute-done((bf16[2304,128]{1,0:T(8,128)(2,1)S(1)}, bf16[2304,128]{1,0:T(8,128)(2,1)S(1)}, u32[]{:S(2)}, u32[]{:S(2)}) %collective-permute-start) | collective-permute-done | bytes 589856 | tf_op jit(solution)/shard_map/ppermute | solution.py:625
  462.6 0.0 copy-start
  462.6 0.6 collective-permute-done.1.first_y
  463.2 0.0 copy-start.1
  463.2 0.0 collective-permute-done.2.last_x
  463.2 0.0 collective-permute-done.3.last_y
  463.2 0.2 copy-done
  463.4 0.6 copy-done.1
  464.0 17.4 %relay.1 = (bf16[8,2304,128]{2,1,0:T(8,128)(2,1)S(1)}, bf16[8,2528,128]{2,1,0:T(8,128)(2,1)S(1)}) custom-call(bf16[2304,128]{1,0:T(8,128)(2,1)} %copy-done, bf16[2304,128]{1,0:T(8,128)(2,1)} %copy-done.1, bf16[2528,128]{1,0:T(8,128)(2,1)S(1)} %collective-permute-done.2.last_x, bf16[2528,128]{1,0:T(8,128)(2,1)S(1)} %collective-permute-done.3.last_y), custom_call_target="tpu_custom_call" | custom-call | tf_op jit(solution)/shard_map/relay/pallas_call | solution.py:547
  481.4 3.2 store_last.1
Async XLA Ops:
  433.1 30.1 %collective-permute-start.2 = (bf16[2528,128]{1,0:T(8,128)(2,1)S(1)}, bf16[2528,128]{1,0:T(8,128)(2,1)S(1)}, u32[]{:S(2)}, u32[]{:S(2)}) collective-permute-start(bf16[2528,128]{1,0:T(8,128)(2,1)S(1)} %get-tuple-element.40), channel_id=1, source_target_pairs={{0,4},{1,5},{2,6},{3,7},{4,0},{5,1},{6,2},{7,3}} | collective-permute-start | bytes 1941512 | tf_op jit(solution)/shard_map/ppermute | solution.py:625
  434.0 29.2 %collective-permute-start.3 = (bf16[2528,128]{1,0:T(8,128)(2,1)S(1)}, bf16[2528,128]{1,0:T(8,128)(2,1)S(1)}, u32[]{:S(2)}, u32[]{:S(2)}) collective-permute-start(bf16[2528,128]{1,0:T(8,128)(2,1)S(1)} %get-tuple-element.40), channel_id=1, source_target_pairs={{0,2},{1,3},{2,0},{3,1},{4,6},{5,7},{6,4},{7,5}} | collective-permute-start | bytes 1941512 | tf_op jit(solution)/shard_map/ppermute | solution.py:625
  435.1 27.4 %collective-permute-start = (bf16[2304,128]{1,0:T(8,128)(2,1)S(1)}, bf16[2304,128]{1,0:T(8,128)(2,1)S(1)}, u32[]{:S(2)}, u32[]{:S(2)}) collective-permute-start(bf16[2304,128]{1,0:T(8,128)(2,1)S(1)} %get-tuple-element.33), channel_id=1, source_target_pairs={{0,4},{1,5},{2,6},{3,7},{4,0},{5,1},{6,2},{7,3}} | collective-permute-start | bytes 1769480 | tf_op jit(solution)/shard_map/ppermute | solution.py:625
  436.0 27.1 %collective-permute-start.1 = (bf16[2304,128]{1,0:T(8,128)(2,1)S(1)}, bf16[2304,128]{1,0:T(8,128)(2,1)S(1)}, u32[]{:S(2)}, u32[]{:S(2)}) collective-permute-start(bf16[2304,128]{1,0:T(8,128)(2,1)S(1)} %get-tuple-element.33), channel_id=1, source_target_pairs={{0,2},{1,3},{2,0},{3,1},{4,6},{5,7},{6,4},{7,5}} | collective-permute-start | bytes 1769480 | tf_op jit(solution)/shard_map/ppermute | solution.py:625
  462.6 0.8 copy-start
  463.2 0.8 copy-start.1

commit v8 on v7

--- a/solution.py
+++ b/solution.py
@@ -396,7 +396,7 @@
     return moments, new_w
 
 
-KINDS = 5
+KINDS = 4
 
 
 def gather_units(layers, block):
@@ -447,7 +447,7 @@
         return across(n, 1, place_of(n, px)), across(n, 2, place_of(n, py))
 
     def distant(n):
-        return tuple(across(n, 3 + half, place_of(n, far, half)) for half in (0, 1))
+        return (across(n, 3, place_of(n, far)),)
 
     def start(copies):
         for copy in copies:
@@ -521,9 +521,9 @@
         )
 
     def distant(n):
-        out = units[n][0]
-        copies = ((4 + 2 * n + half, out.at[far, rows]) for half, rows in enumerate(halves(n)))
-        return tuple(remote(ref, ref, c_send.at[k], c_recv.at[k], pc) for k, ref in copies)
+        out, _, _, base, rows = units[n]
+        ref = out.at[far, pl.ds(base, rows)]
+        return (remote(ref, ref, c_send.at[4 + n], c_recv.at[4 + n], pc),)
 
     settle = [pltpu.make_async_copy(src, first.at[device], settle_sem.at[k]) for k, (src, device) in enumerate(((first_x, px), (first_y, py)))]
     for copy in (*relays(0), *relays(1), *relays(2), *near(), *settle):
@@ -549,7 +549,7 @@
         out_shape=outs,
         in_specs=[HBM] * 4,
         out_specs=[VMEM] * 2,
-        scratch_shapes=[DMA((3,))] * 4 + [DMA((10,))] * 2 + [DMA((2,))],
+        scratch_shapes=[DMA((3,))] * 4 + [DMA((7,))] * 2 + [DMA((2,))],
         compiler_params=pltpu.CompilerParams(collective_id=2, has_side_effects=True, vmem_limit_bytes=2 << 20),
         name="relay",
     )(*(pltpu.with_memory_space_constraint(a, pltpu.HBM) for a in near_first), *near_last)

time: 485 us -> 484 us (level)
  no operation moved by 1% of the time
where the time goes in v8:
time: 484 us
  Pallas kernels  468 us (97%)
  waiting for transfers between devices  10.8 us (2%)
    pallas_call x1, Pallas kernels, scatter(): pl.pallas_call(functools.partial(scatter_kernel, units, half, block), out...  234 us
    pallas_call x1, Pallas kernels, gather(): pl.pallas_call(functools.partial(gather_kernel, units, permuted), out_sha...  187 us
    pallas_call x1, Pallas kernels, relay(): pl.pallas_call(relay_kernel, out_shape=outs, in_specs=[HBM] * 4, out_spec...  17.3 us
    pallas_call x1, Pallas kernels, store(): pl.pallas_call(functools.partial(store_kernel, permuted), out_shape=[jax....  15.2 us
    pallas_call x1, Pallas kernels, adam(): pl.pallas_call(functools.partial(adam_kernel, layers, block), out_shape=[...  11.6 us
    ppermute x4, waiting for transfers between devices, beside(): lax.ppermute(piece, 'dp', [(d, d ^ bit) for d in range(DEVICES)])  10.8 us
  transfers between devices with their start and end apart: 4, of which 2 were waited for; matrix products, arithmetic and copies ran while one was open for 0% of the time, Pallas kernels for 3%

profile of v8, /device:TPU:0, one launch (start us, length us, event | category | flops | bytes accessed | tf_op | source)
XLA Modules:
  0.0 484.3 jit_solution(3539451044664033136)
XLA Ops:
  0.6 233.9 %scatter.1 = (bf16[3,2,4480,128]{3,2,1,0:T(8,128)(2,1)S(1)}, bf16[3,2,4480,128]{3,2,1,0:T(8,128)(2,1)S(1)}, f32[3,2,4480,128]{3,2,1,0:T(8,128)S(1)}, f32[3,2,448...) custom-call(bf16[2,4,2,4480,128]{4,3,2,1,0:T(8,128)(2,1)} %bitcast.107, ...), custom_call_target="tpu_custom_call" | custom-call | tf_op jit(solution)/shard_map/scatter/pallas_call | solution.py:272
  234.6 11.6 %adam.1 = (f32[2,4480,128]{2,1,0:T(8,128)}, f32[2,4480,128]{2,1,0:T(8,128)}, f32[2,4480,128]{2,1,0:T(8,128)}, f32[2,4480,128]{2,1,0:T(8,128)}, f32[2,4480,128]{2...) custom-call(bf16[3,2,4480,128]{3,2,1,0:T(8,128)(2,1)S(1)} %get-tuple-element.34.grad, ...), custom_call_target="tpu_custom_call" | custom-call | flops 17179869184 | bytes 67108864 | tf_op jit(solution)/shard_map/adam/pallas_call | solution.py:379
  246.2 186.8 %gather.1 = (bf16[2,8,4480,128]{3,2,1,0:T(8,128)(2,1)S(1)}, bf16[2,8,4480,128]{3,2,1,0:T(8,128)(2,1)S(1)}, bf16[2,8,4480,128]{3,2,1,0:T(8,128)(2,1)S(1)}, bf16[2528,128]{1,0:T(8,128)(2,1)S(1)}) custom-call(bf16[3,2,4480,128]{3,2,1,0:T(8,128)(2,1)} %get-tuple-element.39.new_w), custom_call_target="tpu_custom_call" | custom-call | tf_op jit(solution)/shard_map/gather/pallas_call | solution.py:487
  432.9 0.9 collective-permute-start.2
  433.8 1.2 collective-permute-start.3
  435.0 0.9 collective-permute-start
  435.9 1.1 collective-permute-start.1
  437.0 15.2 %store.1 = (bf16[2,8,4480,128]{3,2,1,0:T(8,128)(2,1)}, bf16[2,8,4480,128]{3,2,1,0:T(8,128)(2,1)}, bf16[2,8,4480,128]{3,2,1,0:T(8,128)(2,1)}) custom-call(bf16[2,8,4480,128]{3,2,1,0:T(8,128)(2,1)S(1)} %get-tuple-element.43.refs_0_, bf16[2,8,4480,128]{3,2,1,0:T(8,128)(2,1)S(1)} %get-tuple-element.44.refs_1_, ...), custom_call_target="tpu_custom_call" | custom-call | flops 17179869184 | bytes 67108864 | tf_op jit(solution)/shard_map/store/pallas_call | solution.py:587
  452.2 10.2 %collective-permute-done.first_x = bf16[2304,128]{1,0:T(8,128)(2,1)S(1)} collective-permute-done((bf16[2304,128]{1,0:T(8,128)(2,1)S(1)}, bf16[2304,128]{1,0:T(8,128)(2,1)S(1)}, u32[]{:S(2)}, u32[]{:S(2)}) %collective-permute-start) | collective-permute-done | bytes 589856 | tf_op jit(solution)/shard_map/ppermute | solution.py:625
  462.4 0.0 copy-start
  462.4 0.6 collective-permute-done.1.first_y
  463.0 0.0 copy-start.1
  463.0 0.0 collective-permute-done.2.last_x
  463.0 0.0 collective-permute-done.3.last_y
  463.0 0.2 copy-done
  463.2 0.6 copy-done.1
  463.8 17.3 %relay.1 = (bf16[8,2304,128]{2,1,0:T(8,128)(2,1)S(1)}, bf16[8,2528,128]{2,1,0:T(8,128)(2,1)S(1)}) custom-call(bf16[2304,128]{1,0:T(8,128)(2,1)} %copy-done, bf16[2304,128]{1,0:T(8,128)(2,1)} %copy-done.1, bf16[2528,128]{1,0:T(8,128)(2,1)S(1)} %collective-permute-done.2.last_x, bf16[2528,128]{1,0:T(8,128)(2,1)S(1)} %collective-permute-done.3.last_y), custom_call_target="tpu_custom_call" | custom-call | tf_op jit(solution)/shard_map/relay/pallas_call | solution.py:547
  481.2 3.2 store_last.1
Async XLA Ops:
  432.9 30.1 %collective-permute-start.2 = (bf16[2528,128]{1,0:T(8,128)(2,1)S(1)}, bf16[2528,128]{1,0:T(8,128)(2,1)S(1)}, u32[]{:S(2)}, u32[]{:S(2)}) collective-permute-start(bf16[2528,128]{1,0:T(8,128)(2,1)S(1)} %get-tuple-element.40), channel_id=1, source_target_pairs={{0,4},{1,5},{2,6},{3,7},{4,0},{5,1},{6,2},{7,3}} | collective-permute-start | bytes 1941512 | tf_op jit(solution)/shard_map/ppermute | solution.py:625
  433.8 29.2 %collective-permute-start.3 = (bf16[2528,128]{1,0:T(8,128)(2,1)S(1)}, bf16[2528,128]{1,0:T(8,128)(2,1)S(1)}, u32[]{:S(2)}, u32[]{:S(2)}) collective-permute-start(bf16[2528,128]{1,0:T(8,128)(2,1)S(1)} %get-tuple-element.40), channel_id=1, source_target_pairs={{0,2},{1,3},{2,0},{3,1},{4,6},{5,7},{6,4},{7,5}} | collective-permute-start | bytes 1941512 | tf_op jit(solution)/shard_map/ppermute | solution.py:625
  435.0 27.4 %collective-permute-start = (bf16[2304,128]{1,0:T(8,128)(2,1)S(1)}, bf16[2304,128]{1,0:T(8,128)(2,1)S(1)}, u32[]{:S(2)}, u32[]{:S(2)}) collective-permute-start(bf16[2304,128]{1,0:T(8,128)(2,1)S(1)} %get-tuple-element.33), channel_id=1, source_target_pairs={{0,4},{1,5},{2,6},{3,7},{4,0},{5,1},{6,2},{7,3}} | collective-permute-start | bytes 1769480 | tf_op jit(solution)/shard_map/ppermute | solution.py:625
  435.9 27.1 %collective-permute-start.1 = (bf16[2304,128]{1,0:T(8,128)(2,1)S(1)}, bf16[2304,128]{1,0:T(8,128)(2,1)S(1)}, u32[]{:S(2)}, u32[]{:S(2)}) collective-permute-start(bf16[2304,128]{1,0:T(8,128)(2,1)S(1)} %get-tuple-element.33), channel_id=1, source_target_pairs={{0,2},{1,3},{2,0},{3,1},{4,6},{5,7},{6,4},{7,5}} | collective-permute-start | bytes 1769480 | tf_op jit(solution)/shard_map/ppermute | solution.py:625
  462.4 0.8 copy-start
  463.0 0.8 copy-start.1
